TPU v7x, 128 devices: a whole 4x4x4 slice. The times are simulated.
128 devices in a mesh: row: 16 (over y, x), col: 8 (over z, core).
Axes of the slice: x: 4, y: 4, z: 4, core: 2. Of those that a mesh axis runs over, the one named last changes fastest.
Arguments:
- tangents: float32 [192, 128, 6144], P('row', None, 'col'), may hold values from -6 to 6
- base_flow: float32 [192, 128, 192], P('row', None, 'col'), may hold values from -0.0625 to 0.0625
- mode_mask: int32 [192, 192], P('row', 'col'), may hold values 0 or 1
- decay_rates: float32 [128], replicated, may hold values from 1 to 100
- to_eigen: float32 [128, 128], replicated, may hold values from -0.5 to 0.5
- from_eigen: float32 [128, 128], replicated, may hold values from -0.5 to 0.5
Outputs:
- vectors: float32 [192, 128, 6144], P('row', None, 'col')
- growth: float32 [32], replicated
Inputs may be any that keep to these rules, and one draw needn't show every extreme that they name: `mode_mask`: 1 keeps a mode pair of the linearized product, 0 removes it.
All inputs are finite; a program needn't handle non-finite values. No bound on the sum of `mode_mask` on one device may be relied on, other than what follows from the above.
Results may differ from a plain program's by a relative error of at most 0.00005.
Values sent between devices are 32-bit elements; how exact they have to be, the bound alone decides.
A program may use at most 128 MiB of HBM per device.

v0:
```python
import math

import jax
import jax.numpy as jnp
from jax import lax
from jax.sharding import PartitionSpec as P

PRECISE = lax.Precision.HIGHEST
STEP_COEF = 10.0
VISCOSITY = 0.01
ALPHA_X = 0.5
BETA_Z = 1.0


def side_by_side(arrays, axis, split_dim, concat_dim, along):
    widths = [a.shape[along] for a in arrays]
    both = jnp.concatenate(arrays, axis=along)
    out = lax.all_to_all(both, axis, split_axis=split_dim, concat_axis=concat_dim, tiled=True)
    return tuple(jnp.split(out, [sum(widths[:k]) for k in range(1, len(widths))], axis=along))


def total_of_pieces(shard, axis):
    return lax.all_gather(shard, axis).sum(0)


def local_waves(points_count, first_index, length):
    indices = first_index + jnp.arange(length, dtype=jnp.int32)
    middle = points_count // 2
    return jnp.where(indices <= middle, indices, indices - middle).astype(jnp.float32)


def synthesis(points_count):
    points = jnp.arange(points_count, dtype=jnp.int32)[:, None]
    mode_index = jnp.arange(points_count, dtype=jnp.int32)[None, :]
    middle = points_count // 2
    wave_index = jnp.where(mode_index <= middle, mode_index, mode_index - middle)
    turn_count = (points * wave_index % points_count).astype(jnp.float32)
    angles = turn_count * (2.0 * math.pi / points_count)
    return jnp.where(mode_index <= middle, jnp.cos(angles), jnp.sin(angles))


def analysis(points_count):
    mode_index = jnp.arange(points_count, dtype=jnp.int32)
    middle = points_count // 2
    weights = jnp.where(
        (mode_index == 0) | (mode_index == middle),
        jnp.float32(1.0 / points_count),
        jnp.float32(2.0 / points_count),
    )
    return weights[:, None] * synthesis(points_count).T


def derivative_analysis(points_count, wave_scale):
    rows_index = jnp.arange(points_count, dtype=jnp.int32)[:, None]
    cols_index = jnp.arange(points_count, dtype=jnp.int32)[None, :]
    middle = points_count // 2
    rising = (cols_index == rows_index + middle) & (rows_index >= 1) & (rows_index < middle)
    falling = (rows_index == cols_index + middle) & (cols_index >= 1) & (cols_index < middle)
    rows_float = jnp.broadcast_to(rows_index.astype(jnp.float32), (points_count, points_count))
    cols_float = jnp.broadcast_to(cols_index.astype(jnp.float32), (points_count, points_count))
    derivative = jnp.where(rising, rows_float, jnp.float32(0.0)) - jnp.where(
        falling, cols_float, jnp.float32(0.0)
    )
    return -wave_scale * jnp.dot(derivative, analysis(points_count), precision=PRECISE)


def denominators(decay_rates, x_count, z_count, x_start, z_start, x_length, z_length):
    wave_x = ALPHA_X * local_waves(x_count, x_start, x_length)
    wave_z = BETA_Z * local_waves(z_count, z_start, z_length)
    return (
        STEP_COEF
        + VISCOSITY * (wave_x[:, None, None] ** 2 + wave_z[None, None, :] ** 2)
        + decay_rates[None, :, None]
    )


def body(tangents, base_flow, mode_mask, decay_rates, to_eigen, from_eigen):
    x_length, y_count, zv_length = tangents.shape
    z_length = base_flow.shape[2]
    vec_count = zv_length // z_length
    row_devices = lax.axis_size("row")
    col_devices = lax.axis_size("col")
    x_count = x_length * row_devices
    z_count = z_length * col_devices
    x_synthesis = synthesis(x_count)
    z_synthesis = synthesis(z_count)
    x_derivative = derivative_analysis(x_count, ALPHA_X)
    z_analysis = analysis(z_count)
    all_devices = row_devices * col_devices
    plane_count = y_count // all_devices
    stacked = tangents.reshape(x_length, y_count, 1, zv_length)
    speed_stack = base_flow.reshape(x_length, y_count, 1, z_length)
    planes, speed_field = side_by_side((stacked, speed_stack), ("row", "col"), 1, 2, 3)
    x_table = x_synthesis.reshape(x_count, row_devices, x_length)
    z_table = z_synthesis.reshape(z_count, col_devices, z_length)
    planes = planes.reshape(x_length, plane_count, row_devices, col_devices, z_length, vec_count)
    physical = jnp.einsum("myrcnv,prm->ypcnv", planes, x_table, precision=PRECISE)
    physical = jnp.einsum("ypcnv,scn->ypsv", physical, z_table, precision=PRECISE)
    speed_field = speed_field.reshape(x_length, plane_count, row_devices, col_devices, z_length)
    speed_field = jnp.einsum("myrcn,prm->ypcn", speed_field, x_table, precision=PRECISE)
    speed_field = jnp.einsum("ypcn,scn->yps", speed_field, z_table, precision=PRECISE)
    product = physical * speed_field[:, :, :, None]
    returned = jnp.einsum("ypsv,ns->ypnv", product, z_analysis, precision=PRECISE)
    returned = jnp.einsum("ypnv,mp->ymnv", returned, x_derivative, precision=PRECISE)
    returned = returned.reshape(
        plane_count, row_devices, x_length, col_devices, z_length, vec_count
    )
    returned = jnp.transpose(returned, (2, 0, 1, 3, 4, 5)).reshape(
        x_length, plane_count, all_devices, zv_length
    )
    nonlinear = lax.all_to_all(returned, ("row", "col"), split_axis=2, concat_axis=1, tiled=True)
    nonlinear = nonlinear.reshape(x_length, y_count, zv_length)
    x_start = lax.axis_index("row") * x_length
    z_start = lax.axis_index("col") * z_length
    divisor = denominators(decay_rates, x_count, z_count, x_start, z_start, x_length, z_length)
    retained = mode_mask.astype(jnp.float32)[:, None, :, None]
    nonlinear = nonlinear.reshape(x_length, y_count, z_length, vec_count) * retained
    right_side = STEP_COEF * tangents.reshape(x_length, y_count, z_length, vec_count) + nonlinear
    eigen_part = jnp.einsum(
        "ji,mic->mjc", to_eigen, right_side.reshape(x_length, y_count, zv_length), precision=PRECISE
    )
    eigen_part = eigen_part.reshape(x_length, y_count, z_length, vec_count) / divisor[:, :, :, None]
    stepped = jnp.einsum(
        "yj,mjc->myc",
        from_eigen,
        eigen_part.reshape(x_length, y_count, zv_length),
        precision=PRECISE,
    )
    columns = stepped.reshape(x_length * y_count * z_length, vec_count)
    cell_count = x_count * y_count * z_count
    identity = jnp.eye(vec_count, dtype=jnp.float32)
    local_gram = jnp.einsum("cv,cu->vu", columns, columns, precision=PRECISE)
    gram_matrix = total_of_pieces(local_gram, ("row", "col")) / cell_count
    lower_factor = jnp.linalg.cholesky(gram_matrix)
    inverse = jax.scipy.linalg.solve_triangular(lower_factor, identity, lower=True)
    orthonormal = jnp.einsum("cv,uv->cu", columns, inverse, precision=PRECISE)
    growth = jnp.log(jnp.diagonal(lower_factor))
    return (orthonormal.reshape(x_length, y_count, zv_length), growth)


def solution(mesh):
    placed = (P("row", None, "col"), P("row", None, "col"), P("row", "col"), P(), P(), P())
    return jax.shard_map(
        body, mesh=mesh, in_specs=placed, out_specs=(P("row", None, "col"), P()), check_vma=False
    )
```

profile of v0, /device:TPU:1, one launch (start us, length us, event | category | flops | bytes accessed | tf_op | source)
XLA Modules:
  0.0 461.6 jit_solution(4813068991455559650)
XLA Ops:
  1.9 2.7 pad_maximum_fusion
  4.6 6.9 %copy.72 = f32[12,128,1,792]{3,2,0,1:T(1,128)} copy(f32[12,128,1,792]{3,1,0,2:T(8,128)S(1)} %pad_maximum_fusion) | data formatting | bytes 9732096 | tf_op jit(solution)/shard_map/concatenate | solution.py:17
  11.5 11.9 %all-to-all-start = ((f32[12,128,1,792]{3,2,0,1:T(1,128)}), f32[12,128,1,792]{3,2,0,1:T(1,128)}, u32[]{:S(2)}, u32[]{:S(2)}) async-start(f32[12,128,1,792]{3,2,0,1:T(1,128)} %copy.72), calls=%async_computation | async-start | bytes 11010048 | tf_op jit(solution)/shard_map/all_to_all | solution.py:18
  24.9 65.9 %all-to-all-done = f32[12,128,1,792]{3,2,0,1:T(1,128)} async-done(((f32[12,128,1,792]{3,2,0,1:T(1,128)}), f32[12,128,1,792]{3,2,0,1:T(1,128)}, u32[]{:S(2)}, u32[]{:S(2)}) %all-to-all-start) | async-done | bytes 4866080 | tf_op jit(solution)/shard_map/all_to_all | solution.py:18
  90.8 3.0 copy.116
  96.5 12.4 %reshape.260 = f32[12,16,8,24,32]{4,3,2,1,0:T(8,128)} reshape(f32[12,1,128,768]{3,2,0,1:T(8,128)} %split.8) | data formatting | bytes 9437184 | tf_op jit(solution)/shard_map/reshape.8
  108.9 26.0 %copy.74 = f32[12,16,8,24,32]{3,1,0,2,4:T(8,128)} copy(f32[12,16,8,24,32]{4,3,2,1,0:T(8,128)} %reshape.260) | data formatting | bytes 9437184 | tf_op jit(solution)/shard_map/reshape.8
  137.1 46.5 %fusion.23 = f32[192,8,24,32,1]{0,2,4,1,3:T(8,128)S(1)} fusion(f32[12,16,8,24,32]{3,1,0,2,4:T(8,128)} %copy.74, s32[16,12]{0,1:T(8,128)S(1)} %add_select_fusion.3, pred[16,12]{0,1:T(8,128)(4,1)S(1)} %fusion.92), kind=kOutput, calls=%fused_computation.36 | convolution fusion | flops 2718277632 | bytes 9438144 | tf_op jit(solution)/shard_map/myrcnv,prm->ypcnv/dot_general | solution.py:97
  185.0 7.3 %fusion.4 = f32[192,192,32,1]{1,0,3,2:T(8,128)S(1)} fusion(f32[192,8,24,32,1]{0,2,4,1,3:T(8,128)S(1)} %fusion.23, s32[8,24]{1,0:T(8,128)S(1)} %add_select_fusion.4, pred[8,24]{1,0:T(8,128)(4,1)S(1)} %fusion.93), kind=kOutput, calls=%fused_computation.6 | convolution fusion | flops 2718277632 | bytes 9438144 | tf_op jit(solution)/shard_map/ypcnv,scn->ypsv/dot_general | solution.py:98
  192.4 6.6 %fusion.1 = f32[192,192,32]{1,0,2:T(8,128)S(1)} fusion(f32[192,192,32,1]{1,0,3,2:T(8,128)S(1)} %fusion.4, f32[192,192]{0,1:T(8,128)S(1)} %convolution_bitcast_fusion.2, s32[192]{0:T(256)S(1)} %get-tuple-element.4, f32[192]{0:T(256)S(1)} %or_select_fusion, pred[192]{0:T(512)(128)(4,1)S(1)} %get-tuple-element.6), kind=kOutput, calls=%fused_computation.4 | convolution fusion | flops 2719494144 | bytes 9586368 | tf_op jit(solution)/shard_map/ypsv,ns->ypnv/dot_general | solution.py:103
  199.0 17.5 %convolution_bitcast_fusion = f32[12,1,16,8,24,32]{5,2,4,3,0,1:T(8,128)S(1)} fusion(f32[8,24,32,192]{3,1,0,2:T(8,128)S(1)} %bitcast.105, f32[16,12,192,1,1]{2,1,0,4,3:T(8,128)S(1)} %bitcast.110), kind=kOutput, calls=%fused_computation.1 | convolution fusion | flops 2717908992 | bytes 9584640 | tf_op jit(solution)/shard_map/ypnv,mp->ymnv/dot_general | solution.py:104
  216.5 12.1 %copy.99 = f32[12,1,16,8,24,32]{5,4,0,3,2,1:T(8,128)} copy(f32[12,1,16,8,24,32]{5,2,4,3,0,1:T(8,128)S(1)} %convolution_bitcast_fusion) | data formatting | bytes 9437184 | tf_op jit(solution)/shard_map/reshape | solution.py:108
  228.6 15.4 %reshape.286 = f32[12,1,128,768]{3,1,0,2:T(1,128)} reshape(f32[12,1,16,8,24,32]{5,4,0,3,2,1:T(8,128)} %copy.99) | data formatting | bytes 9437184 | tf_op jit(solution)/shard_map/reshape | solution.py:108
  244.1 7.8 %all-to-all-start.1 = ((f32[12,1,128,768]{3,1,0,2:T(1,128)}), f32[12,1,128,768]{3,1,0,2:T(1,128)}, u32[]{:S(2)}, u32[]{:S(2)}) async-start(f32[12,1,128,768]{3,1,0,2:T(1,128)} %reshape.286), calls=%async_computation.1 | async-start | bytes 9437184 | tf_op jit(solution)/shard_map/all_to_all | solution.py:111
  252.4 57.7 %all-to-all-done.1 = f32[12,1,128,768]{3,1,0,2:T(1,128)} async-done(((f32[12,1,128,768]{3,1,0,2:T(1,128)}), f32[12,1,128,768]{3,1,0,2:T(1,128)}, u32[]{:S(2)}, u32[]{:S(2)}) %all-to-all-start.1) | async-done | bytes 4718624 | tf_op jit(solution)/shard_map/all_to_all | solution.py:111
  310.1 10.3 %bitcast_divide_fusion = f32[12,128,768]{1,2,0:T(8,128)S(1)} fusion(f32[12,128,24]{1,2,0:T(8,128)S(1)} %broadcast_add_fusion, f32[128,128]{1,0:T(8,128)S(1)} %copy-done, f32[12,1,128,768]{3,1,0,2:T(1,128)} %all-to-all-done.1, f32[12,128,768]{2,1,0:T(8,128)} %param.6, f32[12,768]{1,0:T(8,128)S(1)} %mul.176), kind=kOutput, calls=%fused_computation.11 | convolution fusion | flops 1816657920 | bytes 14405632 | tf_op jit(solution)/shard_map/ji,mic->mjc/dot_general | solution.py:119
  320.4 5.4 %convolution_bitcast_fusion.1 = f32[12,128,768]{1,2,0:T(8,128)} fusion(f32[12,128,768]{1,2,0:T(8,128)S(1)} %bitcast_divide_fusion, f32[128,128]{1,0:T(8,128)S(1)} %copy-done.1), kind=kOutput, calls=%fused_computation.20 | convolution fusion | flops 1811939328 | bytes 9502720 | tf_op jit(solution)/shard_map/yj,mjc->myc/dot_general | solution.py:123
  325.8 6.1 %copy.84 = f32[12,128,768]{2,1,0:T(8,128)} copy(f32[12,128,768]{1,2,0:T(8,128)} %convolution_bitcast_fusion.1) | data formatting | bytes 9437184 | tf_op jit(solution)/shard_map/yj,mjc->myc/transpose | solution.py:123
  331.9 12.5 %reshape.265 = f32[36864,32]{1,0:T(8,128)} reshape(f32[12,128,768]{2,1,0:T(8,128)} %copy.84) | data formatting | bytes 9437184 | tf_op jit(solution)/shard_map/reshape | solution.py:129
  344.4 38.1 %fusion.119 = f32[32,32]{1,0:T(8,128)S(1)} fusion(f32[36864,32]{1,0:T(8,128)} %reshape.265), kind=kOutput, calls=%fused_computation.162 | convolution fusion | flops 452984832 | bytes 4722688 | tf_op jit(solution)/shard_map/cv,cu->vu/dot_general | solution.py:132
  382.5 36.7 %all-gather = f32[4096,32]{1,0:T(8,128)S(1)} all-gather(f32[32,32]{1,0:T(8,128)S(1)} %fusion.119), channel_id=2, replica_groups=mesh['row'=16,'col'=8] {'row','col'}, dimensions={0}, use_global_device_ids=true | all-gather | bytes 528384 | tf_op jit(solution)/shard_map/all_gather | solution.py:23
  419.5 2.9 cholesky.17
  426.4 20.1 %fusion.120 = f32[36864,32]{1,0:T(8,128)} fusion(f32[36864,32]{1,0:T(8,128)} %reshape.265, f32[32,32]{1,0:T(8,128)S(1)} %fusion.89), kind=kOutput, calls=%fused_computation.163 | convolution fusion | flops 452984832 | bytes 9441280 | tf_op jit(solution)/shard_map/cv,uv->cu/dot_general | solution.py:136
  446.5 13.6 %reshape.266 = f32[12,128,768]{2,1,0:T(8,128)} reshape(f32[36864,32]{1,0:T(8,128)} %fusion.120) | data formatting | bytes 9437184 | tf_op jit(solution)/shard_map/reshape | solution.py:138
  (44 shorter events, 14.8 us)
Async XLA Ops:
  0.6 309.5 %copy-start = (f32[128,128]{1,0:T(8,128)S(1)}, f32[128,128]{1,0:T(8,128)}, u32[]{:S(2)}) copy-start(f32[128,128]{1,0:T(8,128)} %param.10) | copy-start | bytes 196612
  11.5 79.2 %all-to-all-start = ((f32[12,128,1,792]{3,2,0,1:T(1,128)}), f32[12,128,1,792]{3,2,0,1:T(1,128)}, u32[]{:S(2)}, u32[]{:S(2)}) async-start(f32[12,128,1,792]{3,2,0,1:T(1,128)} %copy.72), calls=%async_computation | async-start | bytes 11010048 | tf_op jit(solution)/shard_map/all_to_all | solution.py:18
  244.0 7.8 %copy-start.2 = (s32[12,24]{1,0:T(8,128)S(1)}, s32[12,24]{1,0:T(8,128)}, u32[]{:S(2)}) copy-start(s32[12,24]{1,0:T(8,128)} %param.8) | copy-start | bytes 3460
  244.0 8.2 %copy-start.3 = (f32[128]{0:T(128)S(1)}, f32[128]{0:T(128)}, u32[]{:S(2)}) copy-start(f32[128]{0:T(128)} %param.9) | copy-start | bytes 1540
  244.1 66.0 %all-to-all-start.1 = ((f32[12,1,128,768]{3,1,0,2:T(1,128)}), f32[12,1,128,768]{3,1,0,2:T(1,128)}, u32[]{:S(2)}, u32[]{:S(2)}) async-start(f32[12,1,128,768]{3,1,0,2:T(1,128)} %reshape.286), calls=%async_computation.1 | async-start | bytes 9437184 | tf_op jit(solution)/shard_map/all_to_all | solution.py:111
  252.4 68.0 %copy-start.1 = (f32[128,128]{1,0:T(8,128)S(1)}, f32[128,128]{1,0:T(8,128)}, u32[]{:S(2)}) copy-start(f32[128,128]{1,0:T(8,128)} %param.11) | copy-start | bytes 196612
where the time goes:
time: 469 us; the launch traced here: 462 us
  matrix products  157 us (33%)
  waiting for transfers between devices  124 us (26%)
  local copies, waits for them, and re-layouts  114 us (24%)
  blocking collectives  36.7 us (8%)
  starting transfers between devices  19.7 us (4%)
  other arithmetic  9.9 us (2%)
    all_to_all x1, waiting for transfers between devices, side_by_side(): lax.all_to_all(both, axis, split_axis=split_dim, concat_axis=concat_dim,...  65.9 us
    all_to_all x1, waiting for transfers between devices, body(): lax.all_to_all(returned, ('row', 'col'), split_axis=2, concat_axis=1, til...  57.7 us
    dot_general x1, matrix products, body(): jnp.einsum('myrcnv,prm->ypcnv', planes, x_table, precision=PRECISE)  46.5 us
    another operation x4, local copies, waits for them, and re-layouts  38.6 us
    dot_general x1, matrix products, body(): local_gram = jnp.einsum('cv,cu->vu', columns, columns, precision=PRECISE)  38.1 us
    all_gather x1, blocking collectives, total_of_pieces(): return lax.all_gather(shard, axis).sum(0)  36.7 us
    reshape x2, local copies, waits for them, and re-layouts, body(): jnp.transpose(returned, (2, 0, 1, 3, 4, 5))  27.5 us
    dot_general x1, matrix products, body(): orthonormal = jnp.einsum('cv,uv->cu', columns, inverse, precision=PRECISE)  20.1 us
  transfers between devices with their start and end apart: 2, of which 2 were waited for; matrix products, arithmetic and copies ran while one was open for 0% of the time, Pallas kernels for 0%

commit v1 on v0

--- a/solution.py
+++ b/solution.py
@@ -3,6 +3,8 @@
 import jax
 import jax.numpy as jnp
 from jax import lax
+from jax.experimental import pallas as pl
+from jax.experimental.pallas import tpu as pltpu
 from jax.sharding import PartitionSpec as P
 
 PRECISE = lax.Precision.HIGHEST
@@ -17,6 +19,40 @@
     both = jnp.concatenate(arrays, axis=along)
     out = lax.all_to_all(both, axis, split_axis=split_dim, concat_axis=concat_dim, tiled=True)
     return tuple(jnp.split(out, [sum(widths[:k]) for k in range(1, len(widths))], axis=along))
+
+
+def swap_kernel(x_ref, o_ref, ss, rs, ls):
+    r = lax.axis_index("row")
+    c = lax.axis_index("col")
+    me = r * 8 + c
+    own = pltpu.make_async_copy(x_ref.at[me], o_ref.at[me], ls)
+    own.start()
+
+    def send(k, carry):
+        off = lax.rem(k * 37, 128)
+        r2 = lax.rem(r + off // 8, 16)
+        c2 = lax.rem(c + lax.rem(off, 8), 8)
+        pltpu.make_async_remote_copy(
+            x_ref.at[r2 * 8 + c2], o_ref.at[me], ss, rs,
+            device_id=(r2, c2), device_id_type=pl.DeviceIdType.MESH,
+        ).start()
+        return carry
+
+    lax.fori_loop(1, 128, send, 0)
+    own.wait()
+    pltpu.make_async_copy(x_ref.at[pl.ds(0, 127)], o_ref.at[pl.ds(0, 127)], rs).wait()
+    pltpu.make_async_copy(x_ref.at[pl.ds(0, 127)], o_ref.at[pl.ds(0, 127)], ss).wait()
+
+
+def swap(x):
+    return pl.pallas_call(
+        swap_kernel,
+        out_shape=jax.ShapeDtypeStruct(x.shape, x.dtype),
+        in_specs=[pl.BlockSpec(memory_space=pl.ANY)],
+        out_specs=pl.BlockSpec(memory_space=pl.ANY),
+        scratch_shapes=[pltpu.SemaphoreType.DMA] * 3,
+        compiler_params=pltpu.CompilerParams(has_side_effects=True),
+    )(x)
 
 
 def total_of_pieces(shard, axis):
@@ -90,7 +126,10 @@
     plane_count = y_count // all_devices
     stacked = tangents.reshape(x_length, y_count, 1, zv_length)
     speed_stack = base_flow.reshape(x_length, y_count, 1, z_length)
-    planes, speed_field = side_by_side((stacked, speed_stack), ("row", "col"), 1, 2, 3)
+    speed_field = lax.all_to_all(speed_stack, ("row", "col"), split_axis=1, concat_axis=2, tiled=True)
+    pieces = jnp.transpose(tangents, (1, 0, 2)).reshape(y_count, x_length * zv_length // 128, 128)
+    planes = swap(pieces).reshape(1, all_devices, x_length, zv_length)
+    planes = jnp.transpose(planes, (2, 0, 1, 3))
     x_table = x_synthesis.reshape(x_count, row_devices, x_length)
     z_table = z_synthesis.reshape(z_count, col_devices, z_length)
     planes = planes.reshape(x_length, plane_count, row_devices, col_devices, z_length, vec_count)

time: 469 us -> 497 us (1.060); the launches traced: 462 us -> 496 us
  Pallas kernels: 0 us -> 67.2 us
  waiting for transfers between devices: 124 us -> 57.7 us
  matrix products: 157 us -> 175 us
  local copies, waits for them, and re-layouts: 114 us -> 129 us
    pallas_call x0 -> x1, Pallas kernels: none -> 67.2 us  [swap(): pl.pallas_call(swap_kernel, out_shape=jax.ShapeDtypeStruct(x.shape, x.dty...]
    all_to_all x1, waiting for transfers between devices: 65.9 us -> 0.01 us  [body(): lax.all_to_all(speed_stack, ('row', 'col'), split_axis=1, concat_axis=2,...]
    dot_general x1, matrix products: 46.5 us -> 59.6 us  [body(): jnp.einsum('myrcnv,prm->ypcnv', planes, x_table, precision=PRECISE)]
    unnamed x8 -> x12, local copies, waits for them, and re-layouts: 0.02 us -> 9.2 us
    concatenate x1 -> x0, local copies, waits for them, and re-layouts: 6.93 us -> none  [side_by_side(): both = jnp.concatenate(arrays, axis=along)]
    reshape x0 -> x1, local copies, waits for them, and re-layouts: none -> 6.13 us  [body(): jnp.transpose(tangents, (1, 0, 2))]
    pallas_call x0 -> x1, local copies, waits for them, and re-layouts: none -> 6.09 us  [swap(): pl.pallas_call(swap_kernel, out_shape=jax.ShapeDtypeStruct(x.shape, x.dty...]
    transpose x0 -> x1, local copies, waits for them, and re-layouts: none -> 6.04 us  [body(): planes = jnp.transpose(planes, (2, 0, 1, 3))]
  transfers between devices with their start and end apart: 2 -> 2, of which waited for: 2 -> 1; matrix products, arithmetic and copies ran while one was open for 0% -> 27% of each run, Pallas kernels for 0% -> 14%
where the time goes in v1:
time: 497 us; the launch traced here: 496 us
  matrix products  175 us (35%)
  local copies, waits for them, and re-layouts  129 us (26%)
  Pallas kernels  67.2 us (14%)
  waiting for transfers between devices  57.7 us (12%)
  blocking collectives  36.8 us (7%)
  starting transfers between devices  18 us (4%)
  other arithmetic  10.9 us (2%)
    pallas_call x1, Pallas kernels, swap(): pl.pallas_call(swap_kernel, out_shape=jax.ShapeDtypeStruct(x.shape, x.dty...  67.2 us
    dot_general x1, matrix products, body(): jnp.einsum('myrcnv,prm->ypcnv', planes, x_table, precision=PRECISE)  59.6 us
    all_to_all x1, waiting for transfers between devices, body(): lax.all_to_all(returned, ('row', 'col'), split_axis=2, concat_axis=1, til...  57.7 us
    another operation x3, local copies, waits for them, and re-layouts  38.5 us
    dot_general x1, matrix products, body(): local_gram = jnp.einsum('cv,cu->vu', columns, columns, precision=PRECISE)  37.9 us
    all_gather x1, blocking collectives, total_of_pieces(): return lax.all_gather(shard, axis).sum(0)  36.8 us
    reshape x2, local copies, waits for them, and re-layouts, body(): jnp.transpose(returned, (2, 0, 1, 3, 4, 5))  27.5 us
    dot_general x1, matrix products, body(): orthonormal = jnp.einsum('cv,uv->cu', columns, inverse, precision=PRECISE)  20.1 us
  transfers between devices with their start and end apart: 2, of which 1 were waited for; matrix products, arithmetic and copies ran while one was open for 27% of the time, Pallas kernels for 14%

profile of v1, /device:TPU:1, one launch (start us, length us, event | category | flops | bytes accessed | tf_op | source)
XLA Modules:
  0.0 495.7 jit_solution(9789805490960206931)
XLA Ops:
  7.1 11.5 %all-to-all-start = ((f32[128,1,288]{2,1,0:T(1,128)}), f32[128,1,288]{2,1,0:T(1,128)S(1)}, u32[]{:S(2)}, u32[]{:S(2)}) async-start(f32[128,1,288]{2,1,0:T(1,128)} %reshape.292), calls=%async_computation | async-start | bytes 393216 | tf_op jit(solution)/shard_map/all_to_all | solution.py:129
  18.7 6.0 %copy.67 = f32[12,128,768]{1,2,0:T(8,128)} copy(f32[12,128,768]{2,1,0:T(8,128)} %param.6) | data formatting | bytes 9437184 | tf_op args[0]
  24.7 6.1 %copy.68.x_ref = f32[128,72,128]{2,1,0:T(8,128)} copy(f32[128,72,128]{0,2,1:T(8,128)} %bitcast.112) | data formatting | bytes 9437184 | tf_op jit(solution)/shard_map/reshape | solution.py:130
  30.9 67.2 %shard_map.77 = f32[128,72,128]{2,1,0:T(8,128)} custom-call(f32[128,72,128]{2,1,0:T(8,128)} %copy.68.x_ref), custom_call_target="tpu_custom_call" | custom-call | tf_op jit(solution)/shard_map/pallas_call | solution.py:48
  98.0 6.1 %copy.69 = f32[128,72,128]{0,2,1:T(8,128)} copy(f32[128,72,128]{2,1,0:T(8,128)} %shard_map.77) | data formatting | bytes 9437184 | tf_op jit(solution)/shard_map/pallas_call | solution.py:48
  104.1 6.0 %copy.70 = f32[12,1,128,768]{3,2,0,1:T(8,128)} copy(f32[12,1,128,768]{2,3,0,1:T(8,128)} %bitcast.111) | data formatting | bytes 9437184 | tf_op jit(solution)/shard_map/transpose | solution.py:132
  110.2 12.4 %reshape.264 = f32[12,16,8,24,32]{4,3,2,1,0:T(8,128)} reshape(f32[12,1,128,768]{3,2,0,1:T(8,128)} %copy.70) | data formatting | bytes 9437184 | tf_op jit(solution)/shard_map/reshape.6
  122.6 26.0 %copy.71 = f32[12,16,8,24,32]{3,1,0,2,4:T(8,128)} copy(f32[12,16,8,24,32]{4,3,2,1,0:T(8,128)} %reshape.264) | data formatting | bytes 9437184 | tf_op jit(solution)/shard_map/reshape.6
  148.6 59.6 %fusion.23 = f32[192,8,24,32,1]{0,2,4,1,3:T(8,128)S(1)} fusion(f32[12,16,8,24,32]{3,1,0,2,4:T(8,128)} %copy.71, s32[16,12]{0,1:T(8,128)S(1)} %add_select_fusion.3, pred[16,12]{0,1:T(8,128)(4,1)S(1)} %fusion.92), kind=kOutput, calls=%fused_computation.34 | convolution fusion | flops 2718277632 | bytes 9438144 | tf_op jit(solution)/shard_map/myrcnv,prm->ypcnv/dot_general | solution.py:136
  208.3 9.2 %fusion.4 = f32[192,192,32,1]{1,0,3,2:T(8,128)} fusion(f32[192,8,24,32,1]{0,2,4,1,3:T(8,128)S(1)} %fusion.23, s32[8,24]{1,0:T(8,128)S(1)} %add_select_fusion.4, pred[8,24]{1,0:T(8,128)(4,1)S(1)} %fusion.93), kind=kOutput, calls=%fused_computation.6 | convolution fusion | flops 2718277632 | bytes 9438144 | tf_op jit(solution)/shard_map/ypcnv,scn->ypsv/dot_general | solution.py:137
  225.0 9.1 %fusion.1 = f32[192,192,32]{1,0,2:T(8,128)S(1)} fusion(f32[192,192,32,1]{1,0,3,2:T(8,128)} %fusion.4, f32[192,192]{0,1:T(8,128)S(1)} %convolution_bitcast_fusion.2, s32[192]{0:T(256)S(1)} %get-tuple-element.4, f32[192]{0:T(256)S(1)} %or_select_fusion, pred[192]{0:T(512)(128)(4,1)S(1)} %get-tuple-element.6), kind=kOutput, calls=%fused_computation.4 | convolution fusion | flops 2719494144 | bytes 9586368 | tf_op jit(solution)/shard_map/ypsv,ns->ypnv/dot_general | solution.py:142
  234.1 17.9 %convolution_bitcast_fusion = f32[12,1,16,8,24,32]{5,2,4,3,0,1:T(8,128)S(1)} fusion(f32[8,24,32,192]{3,1,0,2:T(8,128)S(1)} %bitcast.110, f32[16,12,192,1,1]{2,1,0,4,3:T(8,128)S(1)} %bitcast.117), kind=kOutput, calls=%fused_computation.1 | convolution fusion | flops 2717908992 | bytes 9584640 | tf_op jit(solution)/shard_map/ypnv,mp->ymnv/dot_general | solution.py:143
  252.0 11.9 %copy.98 = f32[12,1,16,8,24,32]{5,4,0,3,2,1:T(8,128)} copy(f32[12,1,16,8,24,32]{5,2,4,3,0,1:T(8,128)S(1)} %convolution_bitcast_fusion) | data formatting | bytes 9437184 | tf_op jit(solution)/shard_map/reshape | solution.py:147
  263.9 15.6 %reshape.291 = f32[12,1,128,768]{3,1,0,2:T(1,128)} reshape(f32[12,1,16,8,24,32]{5,4,0,3,2,1:T(8,128)} %copy.98) | data formatting | bytes 9437184 | tf_op jit(solution)/shard_map/reshape | solution.py:147
  279.5 6.6 %all-to-all-start.1 = ((f32[12,1,128,768]{3,1,0,2:T(1,128)}), f32[12,1,128,768]{3,1,0,2:T(1,128)}, u32[]{:S(2)}, u32[]{:S(2)}) async-start(f32[12,1,128,768]{3,1,0,2:T(1,128)} %reshape.291), calls=%async_computation.1 | async-start | bytes 9437184 | tf_op jit(solution)/shard_map/all_to_all | solution.py:150
  286.6 57.7 %all-to-all-done.1 = f32[12,1,128,768]{3,1,0,2:T(1,128)} async-done(((f32[12,1,128,768]{3,1,0,2:T(1,128)}), f32[12,1,128,768]{3,1,0,2:T(1,128)}, u32[]{:S(2)}, u32[]{:S(2)}) %all-to-all-start.1) | async-done | bytes 4718624 | tf_op jit(solution)/shard_map/all_to_all | solution.py:150
  344.3 10.3 %bitcast_divide_fusion = f32[12,128,768]{1,2,0:T(8,128)S(1)} fusion(f32[12,128,24]{1,2,0:T(8,128)S(1)} %broadcast_add_fusion, f32[128,128]{1,0:T(8,128)S(1)} %copy-done, f32[12,1,128,768]{3,1,0,2:T(1,128)} %all-to-all-done.1, f32[12,128,768]{2,1,0:T(8,128)} %param.6, f32[12,768]{1,0:T(8,128)S(1)} %mul.176), kind=kOutput, calls=%fused_computation.9 | convolution fusion | flops 1816657920 | bytes 14405632 | tf_op jit(solution)/shard_map/ji,mic->mjc/dot_general | solution.py:158
  354.6 5.4 %convolution_bitcast_fusion.1 = f32[12,128,768]{1,2,0:T(8,128)} fusion(f32[12,128,768]{1,2,0:T(8,128)S(1)} %bitcast_divide_fusion, f32[128,128]{1,0:T(8,128)S(1)} %copy-done.1), kind=kOutput, calls=%fused_computation.18 | convolution fusion | flops 1811939328 | bytes 9502720 | tf_op jit(solution)/shard_map/yj,mjc->myc/dot_general | solution.py:162
  360.0 6.1 %copy.83 = f32[12,128,768]{2,1,0:T(8,128)} copy(f32[12,128,768]{1,2,0:T(8,128)} %convolution_bitcast_fusion.1) | data formatting | bytes 9437184 | tf_op jit(solution)/shard_map/yj,mjc->myc/transpose | solution.py:162
  366.1 12.5 %reshape.270 = f32[36864,32]{1,0:T(8,128)} reshape(f32[12,128,768]{2,1,0:T(8,128)} %copy.83) | data formatting | bytes 9437184 | tf_op jit(solution)/shard_map/reshape | solution.py:168
  378.6 37.9 %fusion.119 = f32[32,32]{1,0:T(8,128)S(1)} fusion(f32[36864,32]{1,0:T(8,128)} %reshape.270), kind=kOutput, calls=%fused_computation.160 | convolution fusion | flops 452984832 | bytes 4722688 | tf_op jit(solution)/shard_map/cv,cu->vu/dot_general | solution.py:171
  416.4 36.8 %all-gather = f32[4096,32]{1,0:T(8,128)S(1)} all-gather(f32[32,32]{1,0:T(8,128)S(1)} %fusion.119), channel_id=2, replica_groups=mesh['row'=16,'col'=8] {'row','col'}, dimensions={0}, use_global_device_ids=true | all-gather | bytes 528384 | tf_op jit(solution)/shard_map/all_gather | solution.py:59
  460.5 20.1 %fusion.120 = f32[36864,32]{1,0:T(8,128)} fusion(f32[36864,32]{1,0:T(8,128)} %reshape.270, f32[32,32]{1,0:T(8,128)S(1)} %fusion.89), kind=kOutput, calls=%fused_computation.161 | convolution fusion | flops 452984832 | bytes 9441280 | tf_op jit(solution)/shard_map/cv,uv->cu/dot_general | solution.py:175
  480.6 13.6 %reshape.271 = f32[12,128,768]{2,1,0:T(8,128)} reshape(f32[36864,32]{1,0:T(8,128)} %fusion.120) | data formatting | bytes 9437184 | tf_op jit(solution)/shard_map/reshape | solution.py:177
  (50 shorter events, 22.8 us)
Async XLA Ops:
  0.6 343.7 %copy-start = (f32[128,128]{1,0:T(8,128)S(1)}, f32[128,128]{1,0:T(8,128)}, u32[]{:S(2)}) copy-start(f32[128,128]{1,0:T(8,128)} %param.10) | copy-start | bytes 196612
  7.1 211.7 %all-to-all-start = ((f32[128,1,288]{2,1,0:T(1,128)}), f32[128,1,288]{2,1,0:T(1,128)S(1)}, u32[]{:S(2)}, u32[]{:S(2)}) async-start(f32[128,1,288]{2,1,0:T(1,128)} %reshape.292), calls=%async_computation | async-start | bytes 393216 | tf_op jit(solution)/shard_map/all_to_all | solution.py:129
  279.5 6.6 %copy-start.2 = (s32[12,24]{1,0:T(8,128)S(1)}, s32[12,24]{1,0:T(8,128)}, u32[]{:S(2)}) copy-start(s32[12,24]{1,0:T(8,128)} %param.8) | copy-start | bytes 3460
  279.5 6.9 %copy-start.3 = (f32[128]{0:T(128)S(1)}, f32[128]{0:T(128)}, u32[]{:S(2)}) copy-start(f32[128]{0:T(128)} %param.9) | copy-start | bytes 1540
  279.5 64.8 %all-to-all-start.1 = ((f32[12,1,128,768]{3,1,0,2:T(1,128)}), f32[12,1,128,768]{3,1,0,2:T(1,128)}, u32[]{:S(2)}, u32[]{:S(2)}) async-start(f32[12,1,128,768]{3,1,0,2:T(1,128)} %reshape.291), calls=%async_computation.1 | async-start | bytes 9437184 | tf_op jit(solution)/shard_map/all_to_all | solution.py:150
  286.6 68.0 %copy-start.1 = (f32[128,128]{1,0:T(8,128)S(1)}, f32[128,128]{1,0:T(8,128)}, u32[]{:S(2)}) copy-start(f32[128,128]{1,0:T(8,128)} %param.11) | copy-start | bytes 196612

commit v2 on v0

v2 whole, which is shorter than its diff:
```python
import functools
import math

import jax
import jax.numpy as jnp
import numpy as np
from jax import lax
from jax.experimental import pallas as pl
from jax.experimental.pallas import tpu as pltpu
from jax.sharding import PartitionSpec as P

MESH = pl.DeviceIdType.MESH
F32 = jnp.float32
BF16 = jnp.bfloat16
STEP_COEF = 10.0
VISCOSITY = 0.01
ALPHA_X = 0.5
BETA_Z = 1.0

NX = 192
NY = 128
NZ = 192
NV = 32
NR, NC = 16, 8
ND = NR * NC
ML = NX // NR
LANES = 128
LO = LANES // NV
HI = NZ // LO
NH = HI // NC
PIECE = ML * NH
BASE = ML // LO
HOP = 37


def synthesis(n):
    point = np.arange(n)[:, None]
    mode = np.arange(n)[None, :]
    wave = np.where(mode <= n // 2, mode, mode - n // 2)
    angle = (point * wave % n) * (2.0 * math.pi / n)
    return np.where(mode <= n // 2, np.cos(angle), np.sin(angle))


def analysis(n):
    mode = np.arange(n)
    weight = np.where((mode == 0) | (mode == n // 2), 1.0 / n, 2.0 / n)
    return weight[:, None] * synthesis(n).T


def derivative_analysis(n):
    derivative = np.zeros((n, n))
    k = np.arange(1, n // 2)
    derivative[k, n // 2 + k] = k
    derivative[n // 2 + k, k] = -k
    return -ALPHA_X * (derivative @ analysis(n))


def waves(n):
    mode = np.arange(n)
    return np.where(mode <= n // 2, mode, mode - n // 2).astype(np.float32)


def halves(table):
    table = np.asarray(table, np.float32)
    top = table.astype(BF16)
    rest = (table - top.astype(np.float32)).astype(BF16)
    return np.concatenate([top, rest], axis=0)


def mode_slots(tail_first):
    slots = -np.ones((NR, 16), np.int64)
    for r in range(NR):
        for k in range(16):
            if tail_first:
                if k >= 8:
                    slots[r, k] = ML * r + k - 8
                elif k >= 4:
                    slots[r, k] = ML * r + 8 + k - 4
            elif k < ML:
                slots[r, k] = ML * r + k
    return slots.reshape(-1)


def tables():
    low_first = np.arange(NZ).reshape(HI, LO).T.reshape(-1)
    sx, sz = synthesis(NX), synthesis(NZ)
    gx, az = derivative_analysis(NX), analysis(NZ)
    forward, backward = [], []
    for tail_first in (False, True):
        slots = mode_slots(tail_first)
        live = slots >= 0
        w = np.zeros((NX, NR * 16))
        w[:, live] = sx[:, slots[live]]
        forward.append(halves(w))
        g = np.zeros((NR * 16, NX))
        g[live] = gx[slots[live]][:, low_first]
        backward.append(halves(g))
    base_x = np.concatenate([sx[:, low::LO] for low in range(LO)], axis=0)
    top, rest = np.split(halves(base_x), 2)
    base_x3 = np.concatenate([top, rest, top], axis=1)
    base_z = np.zeros((NZ, NC, LO, NV))
    base_z[:, :, :, : NZ // NC] = sz.reshape(NZ, NC, 1, NZ // NC)
    return (
        np.stack(forward),
        np.stack(backward),
        halves(sz[:, low_first]),
        halves(az[low_first]),
        base_x3,
        halves(base_z.reshape(NZ, NC * LANES)),
    )


def split2(x):
    top = x.astype(BF16)
    return top, (x - top.astype(F32)).astype(BF16)


def mm(a, b):
    return jnp.dot(a, b, preferred_element_type=F32)


def mm3(table, x):
    rows = table.shape[0] // 2
    top, rest = split2(x)
    both = mm(table, top)
    return both[:rows] + both[rows:] + mm(table[:rows], rest)


def swap_blocks(parts, lane):
    low_half = lane < 64
    even = (lane // NV) % 2 == 0
    v0, v1, v2, v3 = parts

    def pair(x, y, mask, by):
        return (
            jnp.where(mask, x, pltpu.roll(y, by, 1)),
            jnp.where(mask, pltpu.roll(x, LANES - by, 1), y),
        )

    a0, a2 = pair(v0, v2, low_half, 64)
    a1, a3 = pair(v1, v3, low_half, 64)
    b0, b1 = pair(a0, a1, even, 32)
    b2, b3 = pair(a2, a3, even, 32)
    return b0, b1, b2, b3


def step_kernel(
    q_hbm, base_hbm, mask_ref, wz2_ref, decay_ref, to_ref, from_ref,
    fwd_ref, bwd_ref, sz_ref, az_ref, bx_ref, bz_ref,
    stepped_hbm, inverse_ref, growth_ref,
    q_v, send, recv, mid, speed, land, base_v, base_send, base_recv,
    gram_own, gram_col, gram_row_own, gram_row,
    q_sems, base_sem, out_sems,
    fs, fr, bs, br, rs, rr, cs, cr, ws, wr,
):
    r = lax.axis_index("row")
    c = lax.axis_index("col")
    me = r * NC + c
    my_slot = c * NR + r

    for m in range(ML):
        pltpu.make_async_copy(q_hbm.at[m], q_v.at[m], q_sems.at[m]).start()
    base_copy = pltpu.make_async_copy(base_hbm, base_v, base_sem)
    base_copy.start()

    def partner(k):
        off = lax.rem(k * HOP, ND)
        return lax.rem(r + off // NC, NR), lax.rem(c + lax.rem(off, NC), NC)

    barrier = pltpu.get_barrier_semaphore()

    def greet(k, carry):
        r2, c2 = partner(k)
        pl.semaphore_signal(barrier, inc=1, device_id=(r2, c2), device_id_type=MESH)
        return carry

    lax.fori_loop(1, ND, greet, 0)

    base_copy.wait()
    for high in range(BASE):
        for t in range(NY // 8):
            rows = base_v[high * LO, 8 * t : 8 * t + 8, :]
            for low in range(1, LO):
                rows += pltpu.roll(base_v[high * LO + low, 8 * t : 8 * t + 8, :], NV * low, 1)
            base_send[pl.ds(8 * t * BASE + high, 8, stride=BASE), :] = rows

    def pack(m, carry):
        pltpu.make_async_copy(q_hbm.at[m], q_v.at[m], q_sems.at[m]).wait()
        tail = jnp.where(m < 8, 16 + m, 4 + m)
        for j in range(NH // 2):
            for e, at in ((0, m), (1, tail)):
                tile = 2 * j + e
                for t in range(NY // 8):
                    send[pl.ds(8 * t * PIECE + 24 * j + at, 8, stride=PIECE), :] = q_v[
                        m, 8 * t : 8 * t + 8, tile * LANES : (tile + 1) * LANES
                    ]
        return carry

    lax.fori_loop(0, ML, pack, 0)
    pl.semaphore_wait(barrier, ND - 1)

    def send_base(k, carry):
        r2, c2 = partner(k)
        pltpu.make_async_remote_copy(
            base_send.at[pl.ds((r2 * NC + c2) * BASE, BASE)],
            base_recv.at[pl.ds(my_slot * BASE, BASE)],
            bs, br, device_id=(r2, c2), device_id_type=MESH,
        ).start()
        return carry

    lax.fori_loop(1, ND, send_base, 0)

    def send_piece(k, carry):
        r2, c2 = partner(k)
        pltpu.make_async_remote_copy(
            send.at[pl.ds((r2 * NC + c2) * PIECE, PIECE)],
            recv.at[pl.ds(my_slot * PIECE, PIECE)],
            fs, fr, device_id=(r2, c2), device_id_type=MESH,
        ).start()
        return carry

    lax.fori_loop(1, ND, send_piece, 0)

    base_recv[pl.ds(my_slot * BASE, BASE), :] = base_send[pl.ds(me * BASE, BASE), :]
    recv[pl.ds(my_slot * PIECE, PIECE), :] = send[pl.ds(me * PIECE, PIECE), :]

    def drain(ref, rows, sem):
        part = ref.at[pl.ds(0, (ND - 1) * rows)]
        pltpu.make_async_copy(part, part, sem).wait()

    drain(base_recv, BASE, br)
    lane192 = lax.broadcasted_iota(jnp.int32, (NX, 2 * LANES), 1)
    block = (lane192 // NV) % LO
    speed_t = jnp.zeros((NZ, NX), F32)
    for pair in range(NC // 2):
        field = jnp.concatenate(
            [base_recv[(2 * pair + h) * HI : (2 * pair + h + 1) * HI, :] for h in range(2)], axis=1
        )
        top, rest = split2(field)
        out = mm(bx_ref[...], jnp.concatenate([top, top, rest], axis=0))
        half = jnp.zeros((NX, 2 * LANES), F32)
        for low in range(LO):
            half = jnp.where(block == low, out[low * NX : (low + 1) * NX], half)
        top, rest = split2(half)
        table = bz_ref[:, pair * 2 * LANES : (pair + 1) * 2 * LANES]
        nt = (((1,), (1,)), ((), ()))
        both = lax.dot_general(table, top, nt, preferred_element_type=F32)
        speed_t += both[:NZ] + both[NZ:] + lax.dot_general(
            table[:NZ], rest, nt, preferred_element_type=F32
        )
    speed_parts = jnp.concatenate(split2(speed_t), axis=0)
    point = lax.broadcasted_iota(jnp.int32, (NX, 2 * LANES), 0)

    def spread(i, carry):
        pick = (point == 2 * LO * i + lane192 // NV).astype(F32).astype(BF16)
        both = mm(speed_parts, pick)
        speed[i] = both[:NZ] + both[NZ:]
        return carry

    lax.fori_loop(0, HI // 2, spread, 0)

    drain(recv, PIECE, fr)

    def x_forward(i, carry):
        for e in range(2):
            sides = []
            for h in range(2):
                jj = 2 * i + h
                at = (jj // 3) * (NR * PIECE) + lax.rem(jj, 3) * 24 + 8 * e
                sides.append(
                    jnp.concatenate(
                        [
                            recv[pl.ds(pl.multiple_of(at + PIECE * k, 8), 16), :]
                            for k in range(NR)
                        ],
                        axis=0,
                    )
                )
            out = mm3(fwd_ref[e], jnp.concatenate(sides, axis=1))
            for h in range(2):
                tile = 2 * (2 * i + h) + e
                mid[pl.ds(pl.multiple_of(tile * NX, 8), NX), :] = out[:, h * LANES : (h + 1) * LANES]
        return carry

    lax.fori_loop(0, HI // 4, x_forward, 0)

    lane48 = lax.broadcasted_iota(jnp.int32, (HI, LANES), 1)

    def gathered(ref, first):
        return jnp.concatenate(
            [ref[pl.ds(8 * a * NX + first, 8, stride=NX), :] for a in range(HI // 8)], axis=0
        )

    def z_both(i, carry):
        sides = []
        for h in range(2):
            parts = [gathered(mid, (2 * i + h) * LO + low) for low in range(LO)]
            sides.append(jnp.concatenate(swap_blocks(parts, lane48), axis=0))
        physical = mm3(sz_ref[...], jnp.concatenate(sides, axis=1))
        out = mm3(az_ref[...], physical * speed[i])
        for h in range(2):
            recv[pl.ds(pl.multiple_of((2 * i + h) * NX, 8), NX), :] = out[
                :, h * LANES : (h + 1) * LANES
            ]
        return carry

    lax.fori_loop(0, HI // 2, z_both, 0)

    drain(send, PIECE, fs)

    def x_backward(i, carry):
        outs = []
        for e in range(2):
            sides = []
            for h in range(2):
                tile = 2 * (2 * i + h) + e
                parts = [gathered(recv, low * HI + tile) for low in range(LO)]
                sides.append(jnp.concatenate(swap_blocks(parts, lane48), axis=0))
            outs.append(mm3(bwd_ref[e], jnp.concatenate(sides, axis=1)))
        for h in range(2):
            jj = 2 * i + h
            at = (jj // 3) * PIECE + lax.rem(jj, 3) * 24
            cut = slice(h * LANES, (h + 1) * LANES)
            for k in range(NR):
                first = outs[0][16 * k : 16 * k + 16, cut]
                second = outs[1][16 * k : 16 * k + 16, cut]
                group = jnp.concatenate([first[:8], first[8:] + second[:8], second[8:]], axis=0)
                send[pl.ds(pl.multiple_of(at + k * NC * PIECE, 8), 24), :] = group
        return carry

    lax.fori_loop(0, HI // 4, x_backward, 0)

    def send_back(k, carry):
        r2, c2 = partner(k)
        pltpu.make_async_remote_copy(
            send.at[pl.ds((r2 * NC + c2) * PIECE, PIECE)],
            land.at[pl.ds(me * PIECE, PIECE)],
            rs, rr, device_id=(r2, c2), device_id_type=MESH,
        ).start()
        return carry

    lax.fori_loop(1, ND, send_back, 0)
    land[pl.ds(me * PIECE, PIECE), :] = send[pl.ds(me * PIECE, PIECE), :]
    drain(land, PIECE, rr)

    decay = decay_ref[...]

    def solve(m, carry):
        tail = jnp.where(m < 8, 16 + m, 4 + m)
        mode = r * ML + m
        wave = jnp.where(mode <= NX // 2, mode, mode - NX // 2).astype(F32) * ALPHA_X
        for j in range(NH // 2):
            cut = slice(2 * j * LANES, 2 * (j + 1) * LANES)
            tiles = []
            for at in (m, tail):
                tiles.append(
                    jnp.concatenate(
                        [
                            land[pl.ds(8 * t * PIECE + 24 * j + at, 8, stride=PIECE), :]
                            for t in range(NY // 8)
                        ],
                        axis=0,
                    )
                )
            nonlinear = jnp.concatenate(tiles, axis=1) * mask_ref[m, :, cut]
            right = STEP_COEF * q_v[m, :, cut] + nonlinear
            both = mm(to_ref[...], jnp.concatenate(split2(right), axis=0))
            divisor = (STEP_COEF + VISCOSITY * (wave * wave + wz2_ref[:, cut])) + decay
            eigen = (both[:NY] + both[NY:]) / divisor
            both = mm(from_ref[...], jnp.concatenate(split2(eigen), axis=0))
            q_v[m, :, cut] = both[:NY] + both[NY:]
        pltpu.make_async_copy(q_v.at[m], stepped_hbm.at[m], out_sems.at[m]).start()
        return carry

    lax.fori_loop(0, ML, solve, 0)

    def inner(t, carry):
        at = pl.multiple_of(t * LANES, LANES)
        top, rest = split2(q_v[:, :, pl.ds(at, LANES)].reshape(ML * NY, LANES))
        tn = (((0,), (0,)), ((), ()))
        return carry + lax.dot_general(
            top, jnp.concatenate([top, rest], axis=1), tn, preferred_element_type=F32
        )

    whole = lax.fori_loop(0, NH, inner, jnp.zeros((LANES, 2 * LANES), F32))
    cross = whole[:, LANES:]
    whole = whole[:, :LANES] + cross + cross.T
    own = whole[:NV]
    for low in range(1, LO):
        own += pltpu.roll(whole[NV * low : NV * (low + 1)], LANES - NV * low, 1)
    lane32 = lax.broadcasted_iota(jnp.int32, (NV, LANES), 1)
    own = jnp.where(lane32 < NV, own, 0.0)
    packed = own[:8]
    for k in range(1, NV // 8):
        packed += pltpu.roll(own[8 * k : 8 * k + 8], NV * k, 1)

    gram_own[...] = packed
    gram_col[c] = packed

    def send_col(k, carry):
        pltpu.make_async_remote_copy(
            gram_own, gram_col.at[c], cs, cr,
            device_id=(r, lax.rem(c + k, NC)), device_id_type=MESH,
        ).start()
        return carry

    lax.fori_loop(1, NC, send_col, 0)
    part = gram_col.at[pl.ds(0, NC - 1)]
    pltpu.make_async_copy(part, part, cr).wait()
    total = gram_col[0]
    for k in range(1, NC):
        total += gram_col[k]
    gram_row_own[...] = total
    gram_row[r] = total

    def send_row(k, carry):
        pltpu.make_async_remote_copy(
            gram_row_own, gram_row.at[r], ws, wr,
            device_id=(lax.rem(r + k, NR), c), device_id_type=MESH,
        ).start()
        return carry

    lax.fori_loop(1, NR, send_row, 0)
    part = gram_row.at[pl.ds(0, NR - 1)]
    pltpu.make_async_copy(part, part, wr).wait()
    total = gram_row[0]
    for k in range(1, NR):
        total += gram_row[k]

    gram = jnp.concatenate(
        [total] + [pltpu.roll(total, LANES - NV * k, 1) for k in range(1, NV // 8)], axis=0
    )
    gram = gram / float(NX * NY * NZ)
    row32 = lax.broadcasted_iota(jnp.int32, (NV, LANES), 0)
    work = jnp.where(lane32 < NV, gram, jnp.where(lane32 == row32 + NV, 1.0, 0.0))
    for k in range(NV - 1):
        pivot_row = work[k : k + 1, :]
        factor = work[:, k : k + 1] / work[k : k + 1, k : k + 1]
        work = work - jnp.where(row32 > k, factor, 0.0) * pivot_row
    on_diagonal = jnp.where(lane32 == row32, work, 0.0)
    scale = 1.0 / jnp.sqrt(jnp.sum(on_diagonal, axis=1, keepdims=True))
    inverse = pltpu.roll(jnp.where((lane32 >= NV) & (lane32 < 2 * NV), work, 0.0), LANES - NV, 1) * scale
    inverse_ref[...] = jnp.concatenate(
        [inverse] + [pltpu.roll(inverse, NV * k, 1) for k in range(1, LO)], axis=0
    )
    diagonal = jnp.sum(on_diagonal, axis=0, keepdims=True)
    growth_ref[...] = 0.5 * jnp.log(jnp.where(lane32[:1] < NV, diagonal, 1.0))

    drain(base_send, BASE, bs)
    drain(send, PIECE, rs)
    part = gram_col.at[pl.ds(0, NC - 1)]
    pltpu.make_async_copy(part, part, cs).wait()
    part = gram_row.at[pl.ds(0, NR - 1)]
    pltpu.make_async_copy(part, part, ws).wait()
    for m in range(ML):
        pltpu.make_async_copy(q_v.at[m], stepped_hbm.at[m], out_sems.at[m]).wait()


def turn_kernel(stepped_ref, inverse_ref, out_ref):
    top, rest = split2(inverse_ref[...])
    right = jnp.concatenate([top, rest], axis=0)
    right = jnp.concatenate([right, right], axis=1)
    nt = (((1,), (1,)), ((), ()))
    for t in range(NH):
        cut = slice(t * LANES, (t + 1) * LANES)
        left = jnp.concatenate(split2(stepped_ref[0, :, cut]), axis=1)
        both = lax.dot_general(left, right, nt, preferred_element_type=F32)
        out_ref[0, :, cut] = both[:, :LANES] + both[:, LANES:]


def body(tangents, base_flow, mode_mask, decay_rates, to_eigen, from_eigen):
    zv = tangents.shape[2]
    base_wide = jnp.pad(base_flow, ((0, 0), (0, 0), (0, LANES - base_flow.shape[2])))
    mask_wide = jnp.repeat(mode_mask.astype(F32), NV, axis=1).reshape(ML, 1, zv)
    wz2 = jnp.asarray((BETA_Z * np.repeat(waves(NZ), NV)) ** 2, F32).reshape(NC, zv)
    wz2 = lax.dynamic_slice_in_dim(wz2, lax.axis_index("col"), 1, axis=0)
    decay = decay_rates.reshape(NY, 1)

    def stacked(matrix):
        top = lax.reduce_precision(matrix, exponent_bits=8, mantissa_bits=7)
        rest = lax.reduce_precision(matrix - top, exponent_bits=8, mantissa_bits=7)
        both = jnp.concatenate([top, rest], axis=0).astype(BF16)
        return jnp.concatenate([both, both], axis=1)

    constants = [jnp.asarray(t) for t in tables()]
    vmem = pl.BlockSpec(memory_space=pltpu.VMEM)
    anywhere = pl.BlockSpec(memory_space=pl.ANY)
    rows = ND * PIECE
    dma = pltpu.SemaphoreType.DMA
    stepped, inverse, growth = pl.pallas_call(
        step_kernel,
        out_shape=(
            jax.ShapeDtypeStruct(tangents.shape, F32),
            jax.ShapeDtypeStruct((LANES, LANES), F32),
            jax.ShapeDtypeStruct((1, LANES), F32),
        ),
        in_specs=[anywhere, anywhere] + [vmem] * 11,
        out_specs=(anywhere, vmem, vmem),
        scratch_shapes=[
            pltpu.VMEM(tangents.shape, F32),
            pltpu.VMEM((rows, LANES), F32),
            pltpu.VMEM((rows, LANES), F32),
            pltpu.VMEM((HI * NX, LANES), F32),
            pltpu.VMEM((HI // 2, NZ, 2 * LANES), F32),
            pltpu.VMEM((rows, LANES), F32),
            pltpu.VMEM(base_wide.shape, F32),
            pltpu.VMEM((ND * BASE, LANES), F32),
            pltpu.VMEM((ND * BASE, LANES), F32),
            pltpu.VMEM((8, LANES), F32),
            pltpu.VMEM((NC, 8, LANES), F32),
            pltpu.VMEM((8, LANES), F32),
            pltpu.VMEM((NR, 8, LANES), F32),
            dma((ML,)), dma, dma((ML,)),
        ] + [dma] * 10,
        compiler_params=pltpu.CompilerParams(
            collective_id=0, has_side_effects=True, vmem_limit_bytes=60 * 2**20
        ),
        name="step",
    )(tangents, base_wide, mask_wide, wz2, decay, stacked(to_eigen), stacked(from_eigen), *constants)

    block = pl.BlockSpec((1, NY, zv), lambda m: (m, 0, 0))
    vectors = pl.pallas_call(
        turn_kernel,
        grid=(ML,),
        out_shape=jax.ShapeDtypeStruct(tangents.shape, F32),
        in_specs=[block, pl.BlockSpec((LANES, LANES), lambda m: (0, 0))],
        out_specs=block,
        name="turn",
    )(stepped, inverse)
    return vectors, growth[0, :NV]


def solution(mesh):
    placed = (P("row", None, "col"), P("row", None, "col"), P("row", "col"), P(), P(), P())
    return jax.shard_map(
        body, mesh=mesh, in_specs=placed, out_specs=(P("row", None, "col"), P()), check_vma=False
    )
```

time: 469 us -> 201 us (0.43); the launches traced: 462 us -> 201 us
  Pallas kernels: 0 us -> 191 us
  matrix products: 157 us -> 0 us
  waiting for transfers between devices: 124 us -> 0 us
  local copies, waits for them, and re-layouts: 114 us -> 6.17 us
  blocking collectives: 36.7 us -> 0 us
  starting transfers between devices: 19.7 us -> 0 us
  other arithmetic: 9.9 us -> 3.15 us
    pallas_call x0 -> x2, Pallas kernels: none -> 191 us  [the longest x1 180 us: body(): pl.pallas_call(step_kernel, out_shape=(jax.ShapeDtypeStruct(tangents.shap...]
    dot_general x11 -> x0, matrix products: 157 us -> none  [the longest x1 46.5 us: body(): jnp.einsum('myrcnv,prm->ypcnv', planes, x_table, precision=PRECISE)]
    all_to_all x2 -> x0, waiting for transfers between devices: 124 us -> none  [the longest x1 65.9 us: side_by_side(): lax.all_to_all(both, axis, split_axis=split_dim, concat_axis=concat_dim,...]
    reshape x5 -> x1, local copies, waits for them, and re-layouts: 54.9 us -> 1.37 us  [body(): decay = decay_rates.reshape(NY, 1)]
    another operation x4 -> x1, local copies, waits for them, and re-layouts: 38.6 us -> 0.74 us  [body(): mask_wide = jnp.repeat(mode_mask.astype(F32), NV, axis=1).reshape(ML, 1, zv)]
    all_gather x1 -> x0, blocking collectives: 36.7 us -> none  [total_of_pieces(): return lax.all_gather(shard, axis).sum(0)]
    all_to_all x2 -> x0, starting transfers between devices: 19.7 us -> none  [the longest x1 11.9 us: side_by_side(): lax.all_to_all(both, axis, split_axis=split_dim, concat_axis=concat_dim,...]
    concatenate x1 -> x0, local copies, waits for them, and re-layouts: 6.93 us -> none  [side_by_side(): both = jnp.concatenate(arrays, axis=along)]
  transfers between devices with their start and end apart: 2 -> 0, of which waited for: 2 -> 0; matrix products, arithmetic and copies ran while one was open for 0% -> 0% of each run, Pallas kernels for 0% -> 0%
where the time goes in v2:
time: 201 us
  Pallas kernels  191 us (95%)
  local copies, waits for them, and re-layouts  6.17 us (3%)
  other arithmetic  3.15 us (2%)
    pallas_call x1, Pallas kernels, body(): pl.pallas_call(step_kernel, out_shape=(jax.ShapeDtypeStruct(tangents.shap...  180 us
    pallas_call x1, Pallas kernels, body(): pl.pallas_call(turn_kernel, grid=(ML,), out_shape=jax.ShapeDtypeStruct(ta...  10.6 us

profile of v2, /device:TPU:1, one launch (start us, length us, event | category | flops | bytes accessed | tf_op | source)
XLA Modules:
  0.0 200.8 jit_solution(5304240740934373063)
XLA Ops:
  0.6 1.3 constant_dynamic-slice_fusion.wz2_ref
  2.0 0.7 convert_element_type.4
  2.7 1.4 copy.16.decay_ref
  4.0 0.9 reduce-precision_convert_fusion.1
  4.9 0.9 reduce-precision_convert_fusion
  5.7 0.7 maximum_maximum_fusion
  6.5 0.1 broadcast_in_dim.3
  6.6 0.7 reshape_reshape.3.mask_ref
  7.3 1.2 copy.15
  8.5 1.0 pad.4.base_hbm
  9.5 180.2 %step.1 = (f32[12,128,768]{2,1,0:T(8,128)}, f32[128,128]{1,0:T(8,128)}, f32[1,128]{1,0:T(1,128)}) custom-call(f32[12,128,768]{2,1,0:T(8,128)} %q_hbm.1, f32[12,128,128]{2,1,0:T(8,128)} %pad.4.base_hbm, f32[12,1,768]{2,1,0:T(1,128)} %reshape_reshape.3.mask_ref, f32[1,768]{1,0:T(1,128)} %constant_dynamic-slice_fusion.wz2_ref, f32[128,1]{1,0:T(8,128)} %copy.16.decay_ref, ...), custom_call_target="tpu_custom_call" | custom-call | tf_op jit(solution)/shard_map/step/pallas_call | solution.py:490
  189.7 0.0 copy-start
  189.7 10.6 %turn.1 = f32[12,128,768]{2,1,0:T(8,128)} custom-call(f32[12,128,768]{2,1,0:T(8,128)} %get-tuple-element.5.stepped_ref, f32[128,128]{1,0:T(8,128)} %get-tuple-element.6.inverse_ref), custom_call_target="tpu_custom_call" | custom-call | tf_op jit(solution)/shard_map/turn/pallas_call | solution.py:522
  200.3 0.0 copy-done
  200.3 0.5 slice_bitcast_fusion
Async XLA Ops:
  189.7 10.6 %copy-start = (f32[1,128]{1,0:T(1,128)S(1)}, f32[1,128]{1,0:T(1,128)}, u32[]{:S(2)}) copy-start(f32[1,128]{1,0:T(1,128)} %get-tuple-element.7) | copy-start | bytes 1540

commit v3 on v2

v3 whole, which is shorter than its diff:
```python
import functools
import math

import jax
import jax.numpy as jnp
import numpy as np
from jax import lax
from jax.experimental import pallas as pl
from jax.experimental.pallas import tpu as pltpu
from jax.sharding import PartitionSpec as P

MESH = pl.DeviceIdType.MESH
F32 = jnp.float32
BF16 = jnp.bfloat16
STEP_COEF = 10.0
VISCOSITY = 0.01
ALPHA_X = 0.5
BETA_Z = 1.0

NX = 192
NY = 128
NZ = 192
NV = 32
NR, NC = 16, 8
ND = NR * NC
ML = NX // NR
LANES = 128
LO = LANES // NV
HI = NZ // LO
NH = HI // NC
PIECE = ML * NH
BASE = ML // LO
CHUNKS = NH // 2
PART = PIECE // CHUNKS
SPAN = ND * PART
HOP = 37


def synthesis(n):
    point = np.arange(n)[:, None]
    mode = np.arange(n)[None, :]
    wave = np.where(mode <= n // 2, mode, mode - n // 2)
    angle = (point * wave % n) * (2.0 * math.pi / n)
    return np.where(mode <= n // 2, np.cos(angle), np.sin(angle))


def analysis(n):
    mode = np.arange(n)
    weight = np.where((mode == 0) | (mode == n // 2), 1.0 / n, 2.0 / n)
    return weight[:, None] * synthesis(n).T


def derivative_analysis(n):
    derivative = np.zeros((n, n))
    k = np.arange(1, n // 2)
    derivative[k, n // 2 + k] = k
    derivative[n // 2 + k, k] = -k
    return -ALPHA_X * (derivative @ analysis(n))


def waves(n):
    mode = np.arange(n)
    return np.where(mode <= n // 2, mode, mode - n // 2).astype(np.float32)


def halves(table):
    table = np.asarray(table, np.float32)
    top = table.astype(BF16)
    rest = (table - top.astype(np.float32)).astype(BF16)
    return np.concatenate([top, rest], axis=0)


def mode_slots(tail_first):
    slots = -np.ones((NR, 16), np.int64)
    for r in range(NR):
        for k in range(16):
            if tail_first:
                if k >= 8:
                    slots[r, k] = ML * r + k - 8
                elif k >= 4:
                    slots[r, k] = ML * r + 8 + k - 4
            elif k < ML:
                slots[r, k] = ML * r + k
    return slots.reshape(-1)


def tables():
    low_first = np.arange(NZ).reshape(HI, LO).T.reshape(-1)
    sx, sz = synthesis(NX), synthesis(NZ)
    gx, az = derivative_analysis(NX), analysis(NZ)
    forward, backward = [], []
    for tail_first in (False, True):
        slots = mode_slots(tail_first)
        live = slots >= 0
        w = np.zeros((NX, NR * 16))
        w[:, live] = sx[:, slots[live]]
        forward.append(halves(w))
        g = np.zeros((NR * 16, NX))
        g[live] = gx[slots[live]][:, low_first]
        backward.append(halves(g))
    base_x = np.concatenate([sx[:, low::LO] for low in range(LO)], axis=0)
    top, rest = np.split(halves(base_x), 2)
    base_x3 = np.concatenate([top, rest, top], axis=1)
    base_z = np.zeros((NZ, NC, LO, NV))
    base_z[:, :, :, : NZ // NC] = sz.reshape(NZ, NC, 1, NZ // NC)
    return (
        np.stack(forward),
        np.stack(backward),
        halves(sz[:, low_first]),
        halves(az[low_first]),
        base_x3,
        halves(base_z.reshape(NZ, NC * LANES)),
    )


def split2(x):
    top = x.astype(BF16)
    return top, (x - top.astype(F32)).astype(BF16)


def mm(a, b):
    return jnp.dot(a, b, preferred_element_type=F32)


def mm3(table, x):
    rows = table.shape[0] // 2
    top, rest = split2(x)
    both = mm(table, top)
    return both[:rows] + both[rows:] + mm(table[:rows], rest)


def swap_blocks(parts, lane):
    low_half = lane < 64
    even = (lane // NV) % 2 == 0
    v0, v1, v2, v3 = parts

    def pair(x, y, mask, by):
        return (
            jnp.where(mask, x, pltpu.roll(y, by, 1)),
            jnp.where(mask, pltpu.roll(x, LANES - by, 1), y),
        )

    a0, a2 = pair(v0, v2, low_half, 64)
    a1, a3 = pair(v1, v3, low_half, 64)
    b0, b1 = pair(a0, a1, even, 32)
    b2, b3 = pair(a2, a3, even, 32)
    return b0, b1, b2, b3


def step_kernel(
    q_hbm, base_hbm, mask_hbm, decay_hbm, to_hbm, from_hbm,
    fwd_hbm, bwd_hbm, sz_hbm, az_hbm, bx_hbm, bz_hbm,
    stepped_hbm, inverse_ref, growth_ref,
    q_v, send, recv, mid, speed, land,
    base_v, base_send, base_recv, mask_v, mask_w, decay_v, to_v, from_v, to_s, from_s,
    fwd_v, bwd_v, sz_v, az_v, bx_v, bz_v,
    gram_own, gram_col, gram_row_own, gram_row,
    q_sems, in_sems, out_sems, fr, rr,
    fs, bs, br, rs, cs, cr, ws, wr,
):
    r = lax.axis_index("row")
    c = lax.axis_index("col")
    me = r * NC + c
    my_slot = c * NR + r
    wide = 2 * LANES

    def cut(j):
        return slice(wide * j, wide * (j + 1))

    small = [
        pltpu.make_async_copy(src, dst, in_sems.at[k])
        for k, (src, dst) in enumerate(
            [
                (base_hbm, base_v), (bx_hbm, bx_v), (bz_hbm, bz_v), (fwd_hbm, fwd_v),
                (sz_hbm, sz_v), (az_hbm, az_v), (bwd_hbm, bwd_v), (mask_hbm, mask_v),
                (decay_hbm, decay_v), (to_hbm, to_v), (from_hbm, from_v),
            ]
        )
    ]
    loads = [
        pltpu.make_async_copy(q_hbm.at[:, :, cut(j)], q_v.at[:, :, cut(j)], q_sems.at[j])
        for j in range(CHUNKS)
    ]
    small[0].start()
    for copy in loads:
        copy.start()
    for copy in small[1:]:
        copy.start()

    def partner(k):
        off = lax.rem(k * HOP, ND)
        return lax.rem(r + off // NC, NR), lax.rem(c + lax.rem(off, NC), NC)

    barrier = pltpu.get_barrier_semaphore()

    def greet(k, carry):
        r2, c2 = partner(k)
        pl.semaphore_signal(barrier, inc=1, device_id=(r2, c2), device_id_type=MESH)
        return carry

    lax.fori_loop(1, ND, greet, 0)

    small[0].wait()
    gap = jnp.zeros((NV - NZ // NC, NY), F32)
    for high in range(BASE):
        stack = []
        for low in range(LO):
            stack += [base_v[high * LO + low], gap]
        turned = jnp.concatenate(stack, axis=0).T
        for t in range(NY // 8):
            base_send[pl.ds(8 * t * BASE + high, 8, stride=BASE), :] = turned[8 * t : 8 * t + 8]

    def tail_row(m):
        return jnp.where(m < 8, 16 + m, 4 + m)

    def pack(j):
        loads[j].wait()

        def one(m, carry):
            for e, at in ((0, m), (1, tail_row(m))):
                tile = slice((2 * j + e) * LANES, (2 * j + e + 1) * LANES)
                for t in range(NY // 8):
                    send[pl.ds(j * SPAN + 8 * t * PART + at, 8, stride=PART), :] = q_v[
                        m, 8 * t : 8 * t + 8, tile
                    ]
            return carry

        lax.fori_loop(0, ML, one, 0, unroll=2)

    def send_forward(j):
        def one(k, carry):
            r2, c2 = partner(k)
            pltpu.make_async_remote_copy(
                send.at[pl.ds(j * SPAN + (r2 * NC + c2) * PART, PART)],
                recv.at[pl.ds(j * SPAN + my_slot * PART, PART)],
                fs, fr.at[j], device_id=(r2, c2), device_id_type=MESH,
            ).start()
            return carry

        lax.fori_loop(1, ND, one, 0)

    def send_base(k, carry):
        r2, c2 = partner(k)
        pltpu.make_async_remote_copy(
            base_send.at[pl.ds((r2 * NC + c2) * BASE, BASE)],
            base_recv.at[pl.ds(my_slot * BASE, BASE)],
            bs, br, device_id=(r2, c2), device_id_type=MESH,
        ).start()
        return carry

    pack(0)
    pl.semaphore_wait(barrier, ND - 1)
    lax.fori_loop(1, ND, send_base, 0)
    send_forward(0)
    for j in range(1, CHUNKS):
        pack(j)
        send_forward(j)

    base_recv[pl.ds(my_slot * BASE, BASE), :] = base_send[pl.ds(me * BASE, BASE), :]
    for j in range(CHUNKS):
        recv[pl.ds(j * SPAN + my_slot * PART, PART), :] = send[pl.ds(j * SPAN + me * PART, PART), :]

    def drain(ref, first, rows, sem):
        part = ref.at[pl.ds(first, (ND - 1) * rows)]
        pltpu.make_async_copy(part, part, sem).wait()

    for copy in small[1:]:
        copy.wait()
    for src, dst in ((to_v, to_s), (from_v, from_s)):
        both = jnp.concatenate(split2(src[...]), axis=0)
        dst[...] = jnp.concatenate([both, both], axis=1)
    zv = NZ // NC * NV
    column = lax.broadcasted_iota(jnp.int32, (NZ // NC, zv), 1) // NV
    pick = (lax.broadcasted_iota(jnp.int32, (NZ // NC, zv), 0) == column).astype(F32)
    mask_w[...] = mm(mask_v[...].astype(F32).astype(BF16), pick.astype(BF16))

    drain(base_recv, 0, BASE, br)
    lane192 = lax.broadcasted_iota(jnp.int32, (NX, wide), 1)
    block = (lane192 // NV) % LO
    speed_t = jnp.zeros((NZ, NX), F32)
    nt = (((1,), (1,)), ((), ()))
    for pair in range(NC // 2):
        field = jnp.concatenate(
            [base_recv[(2 * pair + h) * HI : (2 * pair + h + 1) * HI, :] for h in range(2)], axis=1
        )
        top, rest = split2(field)
        out = mm(bx_v[...], jnp.concatenate([top, top, rest], axis=0))
        half = jnp.zeros((NX, wide), F32)
        for low in range(LO):
            half = jnp.where(block == low, out[low * NX : (low + 1) * NX], half)
        top, rest = split2(half)
        table = bz_v[:, cut(pair)]
        both = lax.dot_general(table, top, nt, preferred_element_type=F32)
        speed_t += both[:NZ] + both[NZ:] + lax.dot_general(
            table[:NZ], rest, nt, preferred_element_type=F32
        )
    speed_parts = jnp.concatenate(split2(speed_t), axis=0)
    point = lax.broadcasted_iota(jnp.int32, (NX, wide), 0)

    def spread(i, carry):
        pick = (point == 2 * LO * i + lane192 // NV).astype(F32).astype(BF16)
        both = mm(speed_parts, pick)
        speed[i] = both[:NZ] + both[NZ:]
        return carry

    lax.fori_loop(0, HI // 2, spread, 0)

    def x_forward(j):
        def one(i, carry):
            for e in range(2):
                sides = []
                for h in range(2):
                    at = j * SPAN + (2 * i + h) * (NR * PART) + 8 * e
                    sides.append(
                        jnp.concatenate(
                            [
                                recv[pl.ds(pl.multiple_of(at + PART * k, 8), 16), :]
                                for k in range(NR)
                            ],
                            axis=0,
                        )
                    )
                out = mm3(fwd_v[e], jnp.concatenate(sides, axis=1))
                for h in range(2):
                    tile = NH * (2 * i + h) + 2 * j + e
                    mid[pl.ds(pl.multiple_of(tile * NX, 8), NX), :] = out[
                        :, h * LANES : (h + 1) * LANES
                    ]
            return carry

        lax.fori_loop(0, NC // 2, one, 0, unroll=2)

    for j in range(CHUNKS):
        drain(recv, j * SPAN, PART, fr.at[j])
        x_forward(j)

    lane48 = lax.broadcasted_iota(jnp.int32, (HI, LANES), 1)

    def gathered(ref, first):
        return jnp.concatenate(
            [ref[pl.ds(8 * a * NX + first, 8, stride=NX), :] for a in range(HI // 8)], axis=0
        )

    def z_both(i, carry):
        sides = []
        for h in range(2):
            parts = [gathered(mid, (2 * i + h) * LO + low) for low in range(LO)]
            sides.append(jnp.concatenate(swap_blocks(parts, lane48), axis=0))
        physical = mm3(sz_v[...], jnp.concatenate(sides, axis=1))
        out = mm3(az_v[...], physical * speed[i])
        for h in range(2):
            recv[pl.ds(pl.multiple_of((2 * i + h) * NX, 8), NX), :] = out[
                :, h * LANES : (h + 1) * LANES
            ]
        return carry

    lax.fori_loop(0, HI // 2, z_both, 0, unroll=4)

    def x_backward(j):
        def one(i, carry):
            outs = []
            for e in range(2):
                sides = []
                for h in range(2):
                    tile = NH * (2 * i + h) + 2 * j + e
                    parts = [gathered(recv, low * HI + tile) for low in range(LO)]
                    sides.append(jnp.concatenate(swap_blocks(parts, lane48), axis=0))
                outs.append(mm3(bwd_v[e], jnp.concatenate(sides, axis=1)))
            for h in range(2):
                side = slice(h * LANES, (h + 1) * LANES)
                for k in range(NR):
                    first = outs[0][16 * k : 16 * k + 16, side]
                    second = outs[1][16 * k : 16 * k + 16, side]
                    group = jnp.concatenate(
                        [first[:8], first[8:] + second[:8], second[8:]], axis=0
                    )
                    at = j * SPAN + (k * NC + 2 * i + h) * PART
                    send[pl.ds(pl.multiple_of(at, 8), PART), :] = group
            return carry

        lax.fori_loop(0, NC // 2, one, 0, unroll=2)

    def send_back(j):
        def one(k, carry):
            r2, c2 = partner(k)
            pltpu.make_async_remote_copy(
                send.at[pl.ds(j * SPAN + (r2 * NC + c2) * PART, PART)],
                land.at[pl.ds(j * SPAN + me * PART, PART)],
                rs, rr.at[j], device_id=(r2, c2), device_id_type=MESH,
            ).start()
            return carry

        lax.fori_loop(1, ND, one, 0)

    drain(send, 0, PIECE, fs)
    for j in range(CHUNKS):
        x_backward(j)
        send_back(j)
        land[pl.ds(j * SPAN + me * PART, PART), :] = send[pl.ds(j * SPAN + me * PART, PART), :]

    decay = jnp.broadcast_to(decay_v[...], (NY, NY)).T
    decay = jnp.concatenate([decay, decay], axis=1)

    def wave_of(mode, count):
        return jnp.where(mode <= count // 2, mode, mode - count // 2).astype(F32)

    def solve(j):
        lane = lax.broadcasted_iota(jnp.int32, (1, wide), 1)
        wave_z = BETA_Z * wave_of(c * (NZ // NC) + 2 * LO * j + lane // NV, NZ)
        square_z = wave_z * wave_z

        def one(m, carry):
            wave_x = ALPHA_X * wave_of(r * ML + m, NX)
            tiles = []
            for at in (m, tail_row(m)):
                tiles.append(
                    jnp.concatenate(
                        [
                            land[pl.ds(j * SPAN + 8 * t * PART + at, 8, stride=PART), :]
                            for t in range(NY // 8)
                        ],
                        axis=0,
                    )
                )
            nonlinear = jnp.concatenate(tiles, axis=1) * mask_w[pl.ds(m, 1), cut(j)]
            right = STEP_COEF * q_v[m, :, cut(j)] + nonlinear
            both = mm(to_s[...], jnp.concatenate(split2(right), axis=0))
            divisor = (STEP_COEF + VISCOSITY * (wave_x * wave_x + square_z)) + decay
            eigen = (both[:NY] + both[NY:]) / divisor
            both = mm(from_s[...], jnp.concatenate(split2(eigen), axis=0))
            q_v[m, :, cut(j)] = both[:NY] + both[NY:]
            return carry

        lax.fori_loop(0, ML, one, 0, unroll=3)

    def inner(tile):
        at = slice(tile * LANES, (tile + 1) * LANES)
        top, rest = split2(q_v[:, :, at].reshape(ML * NY, LANES))
        tn = (((0,), (0,)), ((), ()))
        return lax.dot_general(
            top, jnp.concatenate([top, rest], axis=1), tn, preferred_element_type=F32
        )

    stores = [
        pltpu.make_async_copy(q_v.at[:, :, cut(j)], stepped_hbm.at[:, :, cut(j)], out_sems.at[j])
        for j in range(CHUNKS)
    ]
    whole = jnp.zeros((LANES, wide), F32)
    for j in range(CHUNKS):
        drain(land, j * SPAN, PART, rr.at[j])
        solve(j)
        stores[j].start()
        whole += inner(2 * j) + inner(2 * j + 1)

    cross = whole[:, LANES:]
    whole = whole[:, :LANES] + cross + cross.T
    own = whole[:NV]
    for low in range(1, LO):
        own += pltpu.roll(whole[NV * low : NV * (low + 1)], LANES - NV * low, 1)
    lane32 = lax.broadcasted_iota(jnp.int32, (NV, LANES), 1)
    own = jnp.where(lane32 < NV, own, 0.0)
    packed = own[:8]
    for k in range(1, NV // 8):
        packed += pltpu.roll(own[8 * k : 8 * k + 8], NV * k, 1)

    gram_own[...] = packed
    gram_col[c] = packed

    def send_col(k, carry):
        pltpu.make_async_remote_copy(
            gram_own, gram_col.at[c], cs, cr,
            device_id=(r, lax.rem(c + k, NC)), device_id_type=MESH,
        ).start()
        return carry

    lax.fori_loop(1, NC, send_col, 0)
    part = gram_col.at[pl.ds(0, NC - 1)]
    pltpu.make_async_copy(part, part, cr).wait()
    total = gram_col[0]
    for k in range(1, NC):
        total += gram_col[k]
    gram_row_own[...] = total
    gram_row[r] = total

    def send_row(k, carry):
        pltpu.make_async_remote_copy(
            gram_row_own, gram_row.at[r], ws, wr,
            device_id=(lax.rem(r + k, NR), c), device_id_type=MESH,
        ).start()
        return carry

    lax.fori_loop(1, NR, send_row, 0)
    part = gram_row.at[pl.ds(0, NR - 1)]
    pltpu.make_async_copy(part, part, wr).wait()
    total = gram_row[0]
    for k in range(1, NR):
        total += gram_row[k]

    gram = jnp.concatenate(
        [total] + [pltpu.roll(total, LANES - NV * k, 1) for k in range(1, NV // 8)], axis=0
    )
    gram = gram / float(NX * NY * NZ)
    row32 = lax.broadcasted_iota(jnp.int32, (NV, LANES), 0)
    work = jnp.where(lane32 < NV, gram, jnp.where(lane32 == row32 + NV, 1.0, 0.0))
    for k in range(NV - 1):
        pivot_row = work[k : k + 1, :]
        factor = work[:, k : k + 1] / work[k : k + 1, k : k + 1]
        work = work - jnp.where(row32 > k, factor, 0.0) * pivot_row
    on_diagonal = jnp.where(lane32 == row32, work, 0.0)
    scale = 1.0 / jnp.sqrt(jnp.sum(on_diagonal, axis=1, keepdims=True))
    keep = (lane32 >= NV) & (lane32 < 2 * NV)
    inverse = pltpu.roll(jnp.where(keep, work, 0.0), LANES - NV, 1) * scale
    inverse_ref[...] = jnp.concatenate(
        [inverse] + [pltpu.roll(inverse, NV * k, 1) for k in range(1, LO)], axis=0
    )
    diagonal = jnp.sum(on_diagonal, axis=0, keepdims=True)
    growth_ref[...] = 0.5 * jnp.log(jnp.where(lane32[:1] < NV, diagonal, 1.0))

    drain(base_send, 0, BASE, bs)
    drain(send, 0, PIECE, rs)
    part = gram_col.at[pl.ds(0, NC - 1)]
    pltpu.make_async_copy(part, part, cs).wait()
    part = gram_row.at[pl.ds(0, NR - 1)]
    pltpu.make_async_copy(part, part, ws).wait()
    for copy in stores:
        copy.wait()


def turn_kernel(stepped_ref, inverse_ref, growth_ref, out_ref, growth_out):
    top, rest = split2(inverse_ref[...])
    right = jnp.concatenate([top, rest], axis=0)
    right = jnp.concatenate([right, right], axis=1)
    nt = (((1,), (1,)), ((), ()))
    rows = stepped_ref[...].reshape(ML * NY, LANES)
    both = lax.dot_general(
        jnp.concatenate(split2(rows), axis=1), right, nt, preferred_element_type=F32
    )
    out_ref[...] = (both[:, :LANES] + both[:, LANES:]).reshape(ML, NY, LANES)
    growth_out[...] = growth_ref[:, :NV]


def body(tangents, base_flow, mode_mask, decay_rates, to_eigen, from_eigen):
    constants = [jnp.asarray(t) for t in tables()]
    inputs = [
        tangents, jnp.transpose(base_flow, (0, 2, 1)), mode_mask, decay_rates.reshape(1, NY),
        to_eigen, from_eigen,
    ] + constants
    vmem = pl.BlockSpec(memory_space=pltpu.VMEM)
    anywhere = pl.BlockSpec(memory_space=pl.ANY)
    dma = pltpu.SemaphoreType.DMA
    field = pltpu.VMEM((ND * PIECE, LANES), F32)
    stepped, inverse, growth = pl.pallas_call(
        step_kernel,
        out_shape=(
            jax.ShapeDtypeStruct(tangents.shape, F32),
            jax.ShapeDtypeStruct((LANES, LANES), F32),
            jax.ShapeDtypeStruct((1, LANES), F32),
        ),
        in_specs=[anywhere] * len(inputs),
        out_specs=(anywhere, vmem, vmem),
        scratch_shapes=[
            pltpu.VMEM(tangents.shape, F32), field, field, field,
            pltpu.VMEM((HI // 2, NZ, 2 * LANES), F32), field,
            pltpu.VMEM(inputs[1].shape, F32),
            pltpu.VMEM((ND * BASE, LANES), F32),
            pltpu.VMEM((ND * BASE, LANES), F32),
            pltpu.VMEM(mode_mask.shape, jnp.int32),
            pltpu.VMEM((ML, tangents.shape[2]), F32),
            pltpu.VMEM((1, NY), F32),
            pltpu.VMEM((NY, NY), F32),
            pltpu.VMEM((NY, NY), F32),
            pltpu.VMEM((2 * NY, 2 * NY), BF16),
            pltpu.VMEM((2 * NY, 2 * NY), BF16),
        ]
        + [pltpu.VMEM(t.shape, t.dtype) for t in constants]
        + [
            pltpu.VMEM((8, LANES), F32),
            pltpu.VMEM((NC, 8, LANES), F32),
            pltpu.VMEM((8, LANES), F32),
            pltpu.VMEM((NR, 8, LANES), F32),
            dma((CHUNKS,)), dma((len(inputs) - 1,)), dma((CHUNKS,)), dma((CHUNKS,)), dma((CHUNKS,)),
        ]
        + [dma] * 8,
        compiler_params=pltpu.CompilerParams(
            collective_id=0, has_side_effects=True, vmem_limit_bytes=60 * 2**20
        ),
        name="step",
    )(*inputs)

    block = pl.BlockSpec((ML, NY, LANES), lambda t: (0, 0, t))
    vectors, growth = pl.pallas_call(
        turn_kernel,
        grid=(NH,),
        out_shape=(
            jax.ShapeDtypeStruct(tangents.shape, F32),
            jax.ShapeDtypeStruct((1, NV), F32),
        ),
        in_specs=[
            block,
            pl.BlockSpec((LANES, LANES), lambda t: (0, 0)),
            pl.BlockSpec((1, LANES), lambda t: (0, 0)),
        ],
        out_specs=(block, pl.BlockSpec((1, NV), lambda t: (0, 0))),
        name="turn",
    )(stepped, inverse, growth)
    return vectors, growth.reshape(NV)


def solution(mesh):
    placed = (P("row", None, "col"), P("row", None, "col"), P("row", "col"), P(), P(), P())
    return jax.shard_map(
        body, mesh=mesh, in_specs=placed, out_specs=(P("row", None, "col"), P()), check_vma=False
    )
```

time: 201 us -> 158 us (0.79)
  Pallas kernels: 191 us -> 157 us
  local copies, waits for them, and re-layouts: 6.17 us -> 0 us
  other arithmetic: 3.15 us -> 0 us
    pallas_call x1, Pallas kernels: 180 us -> 150 us  [body(): pl.pallas_call(step_kernel, out_shape=(jax.ShapeDtypeStruct(tangents.shap...]
    pallas_call x1, Pallas kernels: 10.6 us -> 7.07 us  [body(): pl.pallas_call(turn_kernel, grid=(NH,), out_shape=(jax.ShapeDtypeStruct(t...]
where the time goes in v3:
time: 158 us
  Pallas kernels  157 us (99%)
    pallas_call x1, Pallas kernels, body(): pl.pallas_call(step_kernel, out_shape=(jax.ShapeDtypeStruct(tangents.shap...  150 us
    pallas_call x1, Pallas kernels, body(): pl.pallas_call(turn_kernel, grid=(NH,), out_shape=(jax.ShapeDtypeStruct(t...  7.07 us

profile of v3, /device:TPU:1, one launch (start us, length us, event | category | flops | bytes accessed | tf_op | source)
XLA Modules:
  0.0 158.0 jit_solution(9339074971933813767)
XLA Ops:
  0.6 150.3 %step.1 = (f32[12,128,768]{2,1,0:T(8,128)}, f32[128,128]{1,0:T(8,128)}, f32[1,128]{1,0:T(1,128)}) custom-call(f32[12,128,768]{2,1,0:T(8,128)} %q_hbm.1, f32[12,24,128]{2,1,0:T(8,128)} %bitcast.3, s32[12,24]{1,0:T(8,128)} %mask_hbm.1, f32[1,128]{1,0:T(1,128)} %bitcast.4, f32[128,128]{1,0:T(8,128)} %to_hbm.1, f32[128,128]{1,0:T(8,128)} %from_hbm.1, ...), custom_call_target="tpu_custom_call" | custom-call | tf_op jit(solution)/shard_map/step/pallas_call | solution.py:552
  151.0 7.1 %turn.1 = (f32[12,128,768]{2,1,0:T(8,128)}, f32[1,32]{1,0:T(1,128)}) custom-call(f32[12,128,768]{2,1,0:T(8,128)} %get-tuple-element.7.stepped_ref, f32[128,128]{1,0:T(8,128)} %get-tuple-element.8.inverse_ref, f32[1,128]{1,0:T(1,128)} %get-tuple-element.9.growth_ref), custom_call_target="tpu_custom_call" | custom-call | tf_op jit(solution)/shard_map/turn/pallas_call | solution.py:591

commit v4 on v3

v4 whole, which is shorter than its diff:
```python
import functools
import math

import jax
import jax.numpy as jnp
import numpy as np
from jax import lax
from jax.experimental import pallas as pl
from jax.experimental.pallas import tpu as pltpu
from jax.sharding import PartitionSpec as P

MESH = pl.DeviceIdType.MESH
F32 = jnp.float32
BF16 = jnp.bfloat16
STEP_COEF = 10.0
VISCOSITY = 0.01
ALPHA_X = 0.5
BETA_Z = 1.0

NX = 192
NY = 128
NZ = 192
NV = 32
NR, NC = 16, 8
ND = NR * NC
ML = NX // NR
NL = NZ // NC
LANES = 128
HALVES = 2
VH = NV // HALVES
LO = LANES // VH
HI = NZ // LO
TILES = HI // NC
PIECE = ML * TILES
PITCH = 40
SPAN = ND * PITCH
EARLY = 24
BLO = LANES // NV
BHI = NX // BLO
BASE = ML // BLO
QUAD = 4
HOP = 37


def synthesis(n):
    point = np.arange(n)[:, None]
    mode = np.arange(n)[None, :]
    wave = np.where(mode <= n // 2, mode, mode - n // 2)
    angle = (point * wave % n) * (2.0 * math.pi / n)
    return np.where(mode <= n // 2, np.cos(angle), np.sin(angle))


def analysis(n):
    mode = np.arange(n)
    weight = np.where((mode == 0) | (mode == n // 2), 1.0 / n, 2.0 / n)
    return weight[:, None] * synthesis(n).T


def derivative_analysis(n):
    derivative = np.zeros((n, n))
    k = np.arange(1, n // 2)
    derivative[k, n // 2 + k] = k
    derivative[n // 2 + k, k] = -k
    return -ALPHA_X * (derivative @ analysis(n))


def waves(n):
    mode = np.arange(n)
    return np.where(mode <= n // 2, mode, mode - n // 2).astype(np.float32)


def halves(table):
    table = np.asarray(table, np.float32)
    top = table.astype(BF16)
    rest = (table - top.astype(np.float32)).astype(BF16)
    return np.concatenate([top, rest], axis=0)


def mode_slots(tail_first):
    slots = -np.ones((NR, 16), np.int64)
    for r in range(NR):
        for k in range(16):
            if tail_first:
                if k >= 8:
                    slots[r, k] = ML * r + k - 8
                elif k >= 4:
                    slots[r, k] = ML * r + 8 + k - 4
            elif k < ML:
                slots[r, k] = ML * r + k
    return slots.reshape(-1)


def spanwise_of(block):
    return block // 2 + 4 * (block % 2)


def tables():
    low, high = np.arange(LO)[:, None], np.arange(HI)[None, :]
    modes = (LO * high + spanwise_of(low)).reshape(-1)
    points = (LO * high + low).reshape(-1)
    sx, sz = synthesis(NX), synthesis(NZ)
    gx, az = derivative_analysis(NX), analysis(NZ)
    forward, backward = [], []
    for tail_first in (False, True):
        slots = mode_slots(tail_first)
        live = slots >= 0
        w = np.zeros((NX, NR * 16))
        w[:, live] = sx[:, slots[live]]
        forward.append(halves(w))
        g = np.zeros((NR * 16, NX))
        g[live] = gx[slots[live]][:, points]
        backward.append(halves(g))
    base_x = np.concatenate([sx[:, k::BLO] for k in range(BLO)], axis=0)
    top, rest = np.split(halves(base_x), 2)
    base_x3 = np.concatenate([top, rest, top], axis=1)
    base_z = np.zeros((NZ, NC, BLO, NV))
    base_z[:, :, :, :NL] = sz.reshape(NZ, NC, 1, NL)
    return (
        np.stack(forward),
        np.stack(backward),
        halves(sz[:, modes]),
        halves(az[modes]),
        base_x3,
        halves(base_z.reshape(NZ, NC * LANES)),
    )


def split2(x):
    top = x.astype(BF16)
    return top, (x - top.astype(F32)).astype(BF16)


def mm(a, b):
    return jnp.dot(a, b, preferred_element_type=F32)


def mm3(table, x):
    rows = table.shape[0] // 2
    top, rest = split2(x)
    both = mm(table, top)
    return both[:rows] + both[rows:] + mm(table[:rows], rest)


def even_blocks(lane, width):
    return (lane // width) % 2 == 0


def pair_up(x, y, lane, width):
    mask = even_blocks(lane, width)
    return (
        jnp.where(mask, x, pltpu.roll(y, width, 1)),
        jnp.where(mask, pltpu.roll(x, LANES - width, 1), y),
    )


def swap_blocks(parts, lane):
    parts = list(parts)
    bit = LO // 2
    while bit:
        for k in range(LO):
            if not k & bit:
                parts[k], parts[k | bit] = pair_up(parts[k], parts[k | bit], lane, VH * bit)
        bit //= 2
    return parts


def step_kernel(
    q_hbm, base_hbm, mask_hbm, decay_hbm, to_hbm, from_hbm,
    fwd_hbm, bwd_hbm, sz_hbm, az_hbm, bx_hbm, bz_hbm,
    stepped_hbm, inverse_ref, growth_ref,
    q_v, send, recv, mid, speed, land,
    base_v, base_send, base_recv, mask_v, mask_w, decay_v, to_v, from_v, to_s, from_s,
    fwd_v, bwd_v, sz_v, az_v, bx_v, bz_v,
    gram_own, gram_col, gram_row_own, gram_row,
    q_sems, in_sems, out_sems, fs, fr, rr,
    bs, br, rs, cs, cr, ws, wr,
):
    r = lax.axis_index("row")
    c = lax.axis_index("col")
    me = r * NC + c
    my_slot = c * NR + r
    wide = 2 * LANES

    def cut(j):
        return slice(wide * j, wide * (j + 1))

    def tile(t):
        return slice(LANES * t, LANES * (t + 1))

    small = [
        pltpu.make_async_copy(src, dst, in_sems.at[k])
        for k, (src, dst) in enumerate(
            [
                (base_hbm, base_v), (bx_hbm, bx_v), (bz_hbm, bz_v), (fwd_hbm, fwd_v),
                (sz_hbm, sz_v), (az_hbm, az_v), (bwd_hbm, bwd_v), (mask_hbm, mask_v),
                (decay_hbm, decay_v), (to_hbm, to_v), (from_hbm, from_v),
            ]
        )
    ]
    loads = [
        pltpu.make_async_copy(q_hbm.at[:, :, cut(j)], q_v.at[:, :, cut(j)], q_sems.at[j])
        for j in range(TILES)
    ]
    small[0].start()
    for copy in loads:
        copy.start()
    for copy in small[1:]:
        copy.start()

    def partner(k):
        off = lax.rem(k * HOP, ND)
        return lax.rem(r + off // NC, NR), lax.rem(c + lax.rem(off, NC), NC)

    barrier = pltpu.get_barrier_semaphore()

    def greet(k, carry):
        r2, c2 = partner(k)
        pl.semaphore_signal(barrier, inc=1, device_id=(r2, c2), device_id_type=MESH)
        return carry

    lax.fori_loop(1, ND, greet, 0)

    def clear(k, carry):
        recv[pl.ds(PITCH * k + PIECE, PITCH - PIECE), :] = jnp.zeros((PITCH - PIECE, LANES), F32)
        return carry

    lax.fori_loop(0, HALVES * ND, clear, 0)

    small[0].wait()
    gap = jnp.zeros((NV - NL, NY), F32)
    for high in range(BASE):
        stack = []
        for low in range(BLO):
            stack += [base_v[high * BLO + low], gap]
        turned = jnp.concatenate(stack, axis=0).T
        for t in range(NY // 8):
            base_send[pl.ds(8 * t * BASE + high, 8, stride=BASE), :] = turned[8 * t : 8 * t + 8]

    def row_of(j, m):
        return (m, jnp.where(m < 8, 16 + m, 4 + m), 24 + m)[j]

    def half_of(first, second, lane, h):
        return pair_up(first, second, lane, VH)[h]

    lane8 = lax.broadcasted_iota(jnp.int32, (8, LANES), 1)

    def pack(h):
        def one(m, carry):
            for j in range(TILES):
                for t in range(NY // 8):
                    rows = slice(8 * t, 8 * t + 8)
                    send[pl.ds(h * SPAN + 8 * t * PITCH + row_of(j, m), 8, stride=PITCH), :] = half_of(
                        q_v[m, rows, tile(2 * j)], q_v[m, rows, tile(2 * j + 1)], lane8, h
                    )
            return carry

        lax.fori_loop(0, ML, one, 0)

    def send_forward(h):
        def one(k, carry):
            r2, c2 = partner(k)
            pltpu.make_async_remote_copy(
                send.at[pl.ds(h * SPAN + (r2 * NC + c2) * PITCH, PIECE)],
                recv.at[pl.ds(h * SPAN + my_slot * PITCH, PIECE)],
                fs.at[h], fr.at[h], device_id=(r2, c2), device_id_type=MESH,
            ).start()
            return carry

        lax.fori_loop(1, ND, one, 0)

    def send_base(k, carry):
        r2, c2 = partner(k)
        pltpu.make_async_remote_copy(
            base_send.at[pl.ds((r2 * NC + c2) * BASE, BASE)],
            base_recv.at[pl.ds(my_slot * BASE, BASE)],
            bs, br, device_id=(r2, c2), device_id_type=MESH,
        ).start()
        return carry

    def keep_own(dst, to, h):
        dst[pl.ds(pl.multiple_of(h * SPAN + to * PITCH, 8), PIECE), :] = send[
            pl.ds(pl.multiple_of(h * SPAN + me * PITCH, 8), PIECE), :
        ]

    for copy in loads:
        copy.wait()
    pack(0)
    pl.semaphore_wait(barrier, ND - 1)
    lax.fori_loop(1, ND, send_base, 0)
    send_forward(0)
    pack(1)
    send_forward(1)
    base_recv[pl.ds(my_slot * BASE, BASE), :] = base_send[pl.ds(me * BASE, BASE), :]
    for h in range(HALVES):
        keep_own(recv, my_slot, h)

    def drain(ref, first, rows, sem):
        part = ref.at[pl.ds(first, (ND - 1) * rows)]
        pltpu.make_async_copy(part, part, sem).wait()

    for copy in small[1:]:
        copy.wait()
    for src, dst in ((to_v, to_s), (from_v, from_s)):
        both = jnp.concatenate(split2(src[...]), axis=0)
        dst[...] = jnp.concatenate([both, both], axis=1)
    spot = lax.broadcasted_iota(jnp.int32, (NL, TILES * LANES), 1) // VH
    column = LO * (spot // LO) + spanwise_of(lax.rem(spot, LO))
    pick = lax.broadcasted_iota(jnp.int32, (NL, TILES * LANES), 0) == column
    retained = mm(mask_v[...].astype(F32).astype(BF16), pick.astype(F32).astype(BF16))
    for j in range(TILES):
        mask_w[16 * j : 16 * j + ML, :] = retained[:, tile(j)]

    drain(base_recv, 0, BASE, br)
    block = (lax.broadcasted_iota(jnp.int32, (NX, wide), 1) // NV) % BLO
    speed_t = jnp.zeros((NZ, NX), F32)
    nt = (((1,), (1,)), ((), ()))
    for pair in range(NC // 2):
        field = jnp.concatenate(
            [base_recv[(2 * pair + h) * BHI : (2 * pair + h + 1) * BHI, :] for h in range(2)],
            axis=1,
        )
        top, rest = split2(field)
        out = mm(bx_v[...], jnp.concatenate([top, top, rest], axis=0))
        half = jnp.zeros((NX, wide), F32)
        for low in range(BLO):
            half = jnp.where(block == low, out[low * NX : (low + 1) * NX], half)
        top, rest = split2(half)
        table = bz_v[:, cut(pair)]
        both = lax.dot_general(table, top, nt, preferred_element_type=F32)
        speed_t += both[:NZ] + both[NZ:] + lax.dot_general(
            table[:NZ], rest, nt, preferred_element_type=F32
        )
    speed_parts = jnp.concatenate(split2(speed_t), axis=0)
    spread_shape = (NX, QUAD * LANES)
    point = lax.broadcasted_iota(jnp.int32, spread_shape, 0)
    spot_x = lax.broadcasted_iota(jnp.int32, spread_shape, 1) // VH

    def spread(i, carry):
        pick = (point == QUAD * LO * i + spot_x).astype(F32).astype(BF16)
        both = mm(speed_parts, pick)
        speed[i] = both[:NZ] + both[NZ:]
        return carry

    lax.fori_loop(0, HI // QUAD, spread, 0)

    types = ((0, (0, 2)), (1, (1,)))
    first_row = (0, 8, 24)

    def x_forward(h):
        def one(i, carry):
            for e, tiles in types:
                at = [(2 * i + k, j) for k in range(2) for j in tiles]
                sides = []
                for c2, j in at:
                    base = h * SPAN + c2 * (NR * PITCH) + first_row[j]
                    sides.append(
                        jnp.concatenate(
                            [
                                recv[pl.ds(pl.multiple_of(base + PITCH * k, 8), 16), :]
                                for k in range(NR)
                            ],
                            axis=0,
                        )
                    )
                out = mm3(fwd_v[e], jnp.concatenate(sides, axis=1))
                for k, (c2, j) in enumerate(at):
                    to = (TILES * c2 + j) * NX
                    mid[pl.ds(pl.multiple_of(to, 8), NX), :] = out[:, tile(k)]
            return carry

        lax.fori_loop(0, NC // 2, one, 0, unroll=2)

    lane24 = lax.broadcasted_iota(jnp.int32, (HI, LANES), 1)

    def gathered(ref, first):
        return jnp.concatenate(
            [ref[pl.ds(8 * a * NX + first, 8, stride=NX), :] for a in range(HI // 8)], axis=0
        )

    def swapped(ref, starts):
        parts = [gathered(ref, first) for first in starts]
        return jnp.concatenate(swap_blocks(parts, lane24), axis=0)

    def z_both(h):
        def one(i, carry):
            sides = [
                swapped(mid, [(QUAD * i + k) * LO + low for low in range(LO)]) for k in range(QUAD)
            ]
            physical = mm3(sz_v[...], jnp.concatenate(sides, axis=1))
            out = mm3(az_v[...], physical * speed[i])
            for k in range(QUAD):
                to = h * SPAN + (QUAD * i + k) * NX
                recv[pl.ds(pl.multiple_of(to, 8), NX), :] = out[:, tile(k)]
            return carry

        lax.fori_loop(0, HI // QUAD, one, 0, unroll=3)

    def x_backward(h):
        def one(i, carry):
            done = {}
            for e, tiles in types:
                at = [(k, j) for k in range(2) for j in tiles]
                sides = []
                for k, j in at:
                    high = TILES * (2 * i + k) + j
                    sides.append(swapped(recv, [h * SPAN + low * HI + high for low in range(LO)]))
                out = mm3(bwd_v[e], jnp.concatenate(sides, axis=1))
                for k, key in enumerate(at):
                    done[key] = out[:, tile(k)]
            for k in range(2):
                for r2 in range(NR):
                    t0, t1, t2 = (done[k, j][16 * r2 : 16 * r2 + 16] for j in range(TILES))
                    to = h * SPAN + (r2 * NC + 2 * i + k) * PITCH
                    send[pl.ds(pl.multiple_of(to, 8), PITCH), :] = jnp.concatenate(
                        [t0[:8], t0[8:] + t1[:8], t1[8:], t2], axis=0
                    )
            return carry

        lax.fori_loop(0, NC // 2, one, 0, unroll=2)

    def send_back(h, first, rows, sem):
        def one(k, carry):
            r2, c2 = partner(k)
            pltpu.make_async_remote_copy(
                send.at[pl.ds(h * SPAN + (r2 * NC + c2) * PITCH + first, rows)],
                land.at[pl.ds(h * SPAN + me * PITCH + first, rows)],
                rs, sem, device_id=(r2, c2), device_id_type=MESH,
            ).start()
            return carry

        lax.fori_loop(1, ND, one, 0)

    for h in range(HALVES):
        drain(recv, h * SPAN, PIECE, fr.at[h])
        x_forward(h)
        z_both(h)
        drain(send, h * SPAN, PIECE, fs.at[h])
        x_backward(h)
        if h < HALVES - 1:
            send_back(h, 0, PIECE, rr.at[0])
        else:
            send_back(h, 0, EARLY, rr.at[1])
            send_back(h, EARLY, PIECE - EARLY, rr.at[2])
        keep_own(land, me, h)

    decay = jnp.broadcast_to(decay_v[...], (NY, NY)).T
    decay = jnp.concatenate([decay, decay], axis=1)
    lane128 = lax.broadcasted_iota(jnp.int32, (NY, LANES), 1)
    spot = lax.broadcasted_iota(jnp.int32, (1, LANES), 1) // VH

    def wave_of(mode, count):
        return jnp.where(mode <= count // 2, mode, mode - count // 2).astype(F32)

    def solve(h, j):
        wave_z = BETA_Z * wave_of(c * NL + LO * j + spanwise_of(spot), NZ)
        square_z = wave_z * wave_z

        def one(i, carry):
            right, squares = [], []
            for m in (2 * i, 2 * i + 1):
                nonlinear = jnp.concatenate(
                    [
                        land[pl.ds(h * SPAN + 8 * t * PITCH + row_of(j, m), 8, stride=PITCH), :]
                        for t in range(NY // 8)
                    ],
                    axis=0,
                )
                field = half_of(q_v[m, :, tile(2 * j)], q_v[m, :, tile(2 * j + 1)], lane128, h)
                right.append(STEP_COEF * field + nonlinear * mask_w[pl.ds(16 * j + m, 1), :])
                wave_x = ALPHA_X * wave_of(r * ML + m, NX)
                squares.append(wave_x * wave_x + square_z)
            right = jnp.concatenate(right, axis=1)
            both = mm(to_s[...], jnp.concatenate(split2(right), axis=0))
            divisor = (STEP_COEF + VISCOSITY * jnp.concatenate(squares, axis=1)) + decay
            eigen = (both[:NY] + both[NY:]) / divisor
            both = mm(from_s[...], jnp.concatenate(split2(eigen), axis=0))
            stepped = both[:NY] + both[NY:]
            for k, m in enumerate((2 * i, 2 * i + 1)):
                kept = pl.ds(pl.multiple_of((j * ML + m) * NY, 8), NY)
                if h < HALVES - 1:
                    mid[kept, :] = stepped[:, tile(k)]
                else:
                    first, second = pair_up(mid[kept, :], stepped[:, tile(k)], lane128, VH)
                    q_v[m, :, tile(2 * j)] = first
                    q_v[m, :, tile(2 * j + 1)] = second
            return carry

        lax.fori_loop(0, ML // 2, one, 0, unroll=3)

    def inner(t):
        top, rest = split2(q_v[:, :, tile(t)].reshape(ML * NY, LANES))
        tn = (((0,), (0,)), ((), ()))
        return lax.dot_general(
            top, jnp.concatenate([top, rest], axis=1), tn, preferred_element_type=F32
        )

    stores = [
        pltpu.make_async_copy(q_v.at[:, :, cut(j)], stepped_hbm.at[:, :, cut(j)], out_sems.at[j])
        for j in range(TILES)
    ]
    drain(land, 0, PIECE, rr.at[0])
    for j in range(TILES):
        solve(0, j)
    whole = jnp.zeros((LANES, wide), F32)
    for j in range(TILES):
        if j == 0:
            drain(land, SPAN, EARLY, rr.at[1])
        if j == TILES - 1:
            drain(land, SPAN, PIECE - EARLY, rr.at[2])
        solve(1, j)
        stores[j].start()
        whole += inner(2 * j) + inner(2 * j + 1)

    cross = whole[:, LANES:]
    whole = whole[:, :LANES] + cross + cross.T
    own = whole[:NV]
    for low in range(1, BLO):
        own += pltpu.roll(whole[NV * low : NV * (low + 1)], LANES - NV * low, 1)
    lane32 = lax.broadcasted_iota(jnp.int32, (NV, LANES), 1)
    own = jnp.where(lane32 < NV, own, 0.0)
    packed = own[:8]
    for k in range(1, NV // 8):
        packed += pltpu.roll(own[8 * k : 8 * k + 8], NV * k, 1)

    gram_own[...] = packed
    gram_col[c] = packed

    def send_col(k, carry):
        pltpu.make_async_remote_copy(
            gram_own, gram_col.at[c], cs, cr,
            device_id=(r, lax.rem(c + k, NC)), device_id_type=MESH,
        ).start()
        return carry

    lax.fori_loop(1, NC, send_col, 0)
    part = gram_col.at[pl.ds(0, NC - 1)]
    pltpu.make_async_copy(part, part, cr).wait()
    total = gram_col[0]
    for k in range(1, NC):
        total += gram_col[k]
    gram_row_own[...] = total
    gram_row[r] = total

    def send_row(k, carry):
        pltpu.make_async_remote_copy(
            gram_row_own, gram_row.at[r], ws, wr,
            device_id=(lax.rem(r + k, NR), c), device_id_type=MESH,
        ).start()
        return carry

    lax.fori_loop(1, NR, send_row, 0)
    part = gram_row.at[pl.ds(0, NR - 1)]
    pltpu.make_async_copy(part, part, wr).wait()
    total = gram_row[0]
    for k in range(1, NR):
        total += gram_row[k]

    gram = jnp.concatenate(
        [total] + [pltpu.roll(total, LANES - NV * k, 1) for k in range(1, NV // 8)], axis=0
    )
    gram = gram / float(NX * NY * NZ)
    row32 = lax.broadcasted_iota(jnp.int32, (NV, LANES), 0)
    work = jnp.where(lane32 < NV, gram, jnp.where(lane32 == row32 + NV, 1.0, 0.0))
    for k in range(NV - 1):
        pivot_row = work[k : k + 1, :]
        factor = work[:, k : k + 1] / work[k : k + 1, k : k + 1]
        work = work - jnp.where(row32 > k, factor, 0.0) * pivot_row
    on_diagonal = jnp.where(lane32 == row32, work, 0.0)
    scale = 1.0 / jnp.sqrt(jnp.sum(on_diagonal, axis=1, keepdims=True))
    keep = (lane32 >= NV) & (lane32 < 2 * NV)
    inverse = pltpu.roll(jnp.where(keep, work, 0.0), LANES - NV, 1) * scale
    inverse_ref[...] = jnp.concatenate(
        [inverse] + [pltpu.roll(inverse, NV * k, 1) for k in range(1, BLO)], axis=0
    )
    diagonal = jnp.sum(on_diagonal, axis=0, keepdims=True)
    growth_ref[...] = 0.5 * jnp.log(jnp.where(lane32[:1] < NV, diagonal, 1.0))

    drain(base_send, 0, BASE, bs)
    drain(send, 0, HALVES * PIECE, rs)
    part = gram_col.at[pl.ds(0, NC - 1)]
    pltpu.make_async_copy(part, part, cs).wait()
    part = gram_row.at[pl.ds(0, NR - 1)]
    pltpu.make_async_copy(part, part, ws).wait()
    for copy in stores:
        copy.wait()


def turn_kernel(stepped_hbm, inverse_ref, growth_ref, out_hbm, growth_out, x_v, y_v, in_sems, out_sems):
    def load(t):
        at = pl.ds(pl.multiple_of(t * LANES, LANES), LANES)
        return pltpu.make_async_copy(stepped_hbm.at[:, :, at], x_v.at[t], in_sems.at[t])

    def store(t):
        at = pl.ds(pl.multiple_of(t * LANES, LANES), LANES)
        return pltpu.make_async_copy(y_v.at[t], out_hbm.at[:, :, at], out_sems.at[t])

    count = x_v.shape[0]
    for t in range(count):
        load(t).start()
    top, rest = split2(inverse_ref[...])
    right = jnp.concatenate([top, rest], axis=0)
    right = jnp.concatenate([right, right], axis=1)
    growth_out[...] = growth_ref[:, :NV]

    def one(t, carry):
        load(t).wait()
        nt = (((1,), (1,)), ((), ()))
        rows = x_v[t].reshape(ML * NY, LANES)
        both = lax.dot_general(
            jnp.concatenate(split2(rows), axis=1), right, nt, preferred_element_type=F32
        )
        y_v[t] = (both[:, :LANES] + both[:, LANES:]).reshape(ML, NY, LANES)
        store(t).start()
        return carry

    lax.fori_loop(0, count, one, 0)
    for t in range(count):
        store(t).wait()


def body(tangents, base_flow, mode_mask, decay_rates, to_eigen, from_eigen):
    constants = [jnp.asarray(t) for t in tables()]
    inputs = [
        tangents, jnp.transpose(base_flow, (0, 2, 1)), mode_mask, decay_rates.reshape(1, NY),
        to_eigen, from_eigen,
    ] + constants
    vmem = pl.BlockSpec(memory_space=pltpu.VMEM)
    anywhere = pl.BlockSpec(memory_space=pl.ANY)
    dma = pltpu.SemaphoreType.DMA
    field = pltpu.VMEM((HALVES * SPAN, LANES), F32)
    stepped, inverse, growth = pl.pallas_call(
        step_kernel,
        out_shape=(
            jax.ShapeDtypeStruct(tangents.shape, F32),
            jax.ShapeDtypeStruct((LANES, LANES), F32),
            jax.ShapeDtypeStruct((1, LANES), F32),
        ),
        in_specs=[anywhere] * len(inputs),
        out_specs=(anywhere, vmem, vmem),
        scratch_shapes=[
            pltpu.VMEM(tangents.shape, F32), field, field,
            pltpu.VMEM((HI * NX, LANES), F32),
            pltpu.VMEM((HI // QUAD, NZ, QUAD * LANES), F32), field,
            pltpu.VMEM(inputs[1].shape, F32),
            pltpu.VMEM((ND * BASE, LANES), F32),
            pltpu.VMEM((ND * BASE, LANES), F32),
            pltpu.VMEM(mode_mask.shape, jnp.int32),
            pltpu.VMEM((16 * TILES, LANES), F32),
            pltpu.VMEM((1, NY), F32),
            pltpu.VMEM((NY, NY), F32),
            pltpu.VMEM((NY, NY), F32),
            pltpu.VMEM((2 * NY, 2 * NY), BF16),
            pltpu.VMEM((2 * NY, 2 * NY), BF16),
        ]
        + [pltpu.VMEM(t.shape, t.dtype) for t in constants]
        + [
            pltpu.VMEM((8, LANES), F32),
            pltpu.VMEM((NC, 8, LANES), F32),
            pltpu.VMEM((8, LANES), F32),
            pltpu.VMEM((NR, 8, LANES), F32),
            dma((TILES,)), dma((len(inputs) - 1,)), dma((TILES,)),
            dma((HALVES,)), dma((HALVES,)), dma((3,)),
        ]
        + [dma] * 7,
        compiler_params=pltpu.CompilerParams(
            collective_id=0, has_side_effects=True, vmem_limit_bytes=60 * 2**20
        ),
        name="step",
    )(*inputs)

    tiles = tangents.shape[2] // LANES
    vectors, growth = pl.pallas_call(
        turn_kernel,
        out_shape=(
            jax.ShapeDtypeStruct(tangents.shape, F32),
            jax.ShapeDtypeStruct((1, NV), F32),
        ),
        in_specs=[anywhere, vmem, vmem],
        out_specs=(anywhere, vmem),
        scratch_shapes=[
            pltpu.VMEM((tiles, ML, NY, LANES), F32),
            pltpu.VMEM((tiles, ML, NY, LANES), F32),
            dma((tiles,)), dma((tiles,)),
        ],
        compiler_params=pltpu.CompilerParams(vmem_limit_bytes=40 * 2**20),
        name="turn",
    )(stepped, inverse, growth)
    return vectors, growth.reshape(NV)


def solution(mesh):
    placed = (P("row", None, "col"), P("row", None, "col"), P("row", "col"), P(), P(), P())
    return jax.shard_map(
        body, mesh=mesh, in_specs=placed, out_specs=(P("row", None, "col"), P()), check_vma=False
    )
```

time: 158 us -> 144 us (0.911)
  Pallas kernels: 157 us -> 139 us
  local copies, waits for them, and re-layouts: 0 us -> 3.84 us
    pallas_call x1, Pallas kernels: 150 us -> 135 us  [body(): pl.pallas_call(step_kernel, out_shape=(jax.ShapeDtypeStruct(tangents.shap...]
    unnamed x0 -> x6, local copies, waits for them, and re-layouts: none -> 3.84 us
    pallas_call x1, Pallas kernels: 7.07 us -> 4.34 us  [body(): pl.pallas_call(turn_kernel, out_shape=(jax.ShapeDtypeStruct(tangents.shap...]
where the time goes in v4:
time: 144 us
  Pallas kernels  139 us (97%)
  local copies, waits for them, and re-layouts  3.84 us (3%)
    pallas_call x1, Pallas kernels, body(): pl.pallas_call(step_kernel, out_shape=(jax.ShapeDtypeStruct(tangents.shap...  135 us
    pallas_call x1, Pallas kernels, body(): pl.pallas_call(turn_kernel, out_shape=(jax.ShapeDtypeStruct(tangents.shap...  4.34 us
    unnamed x6, local copies, waits for them, and re-layouts  3.84 us

profile of v4, /device:TPU:1, one launch (start us, length us, event | category | flops | bytes accessed | tf_op | source)
XLA Modules:
  0.0 144.0 jit_solution(2605050621499590150)
XLA Ops:
  0.6 135.0 %step.1 = (f32[12,128,768]{2,1,0:T(8,128)}, f32[128,128]{1,0:T(8,128)}, f32[1,128]{1,0:T(1,128)}) custom-call(f32[12,128,768]{2,1,0:T(8,128)} %q_hbm.1, f32[12,24,128]{2,1,0:T(8,128)} %bitcast.3, s32[12,24]{1,0:T(8,128)} %mask_hbm.1, f32[1,128]{1,0:T(1,128)} %bitcast.4, f32[128,128]{1,0:T(8,128)} %to_hbm.1, f32[128,128]{1,0:T(8,128)} %from_hbm.1, ...), custom_call_target="tpu_custom_call" | custom-call | tf_op jit(solution)/shard_map/step/pallas_call | solution.py:631
  135.6 0.0 copy-start
  135.6 2.3 %copy-done = f32[12,128,768]{2,1,0:T(8,128)S(1)} copy-done((f32[12,128,768]{2,1,0:T(8,128)S(1)}, f32[12,128,768]{2,1,0:T(8,128)}, u32[]{:S(2)}) %copy-start) | copy-done | bytes 4718616
  138.0 0.0 copy-start.1
  138.0 0.8 copy-done.1
  138.8 0.0 copy-start.2
  138.8 0.7 copy-done.2
  139.5 4.3 %turn.1 = (f32[12,128,768]{2,1,0:T(8,128)}, f32[1,32]{1,0:T(1,128)}) custom-call(f32[12,128,768]{2,1,0:T(8,128)S(1)} %copy-done, f32[128,128]{1,0:T(8,128)S(1)} %copy-done.1, f32[1,128]{1,0:T(1,128)S(1)} %copy-done.2), custom_call_target="tpu_custom_call" | custom-call | tf_op jit(solution)/shard_map/turn/pallas_call | solution.py:672
Async XLA Ops:
  135.6 2.3 %copy-start = (f32[12,128,768]{2,1,0:T(8,128)S(1)}, f32[12,128,768]{2,1,0:T(8,128)}, u32[]{:S(2)}) copy-start(f32[12,128,768]{2,1,0:T(8,128)} %get-tuple-element.7.stepped_hbm) | copy-start | bytes 14155780
  138.0 0.8 copy-start.1
  138.8 0.7 copy-start.2

commit v5 on v4

--- a/solution.py
+++ b/solution.py
@@ -39,7 +39,7 @@
 BHI = NX // BLO
 BASE = ML // BLO
 QUAD = 4
-HOP = 37
+HOP = 101
 
 
 def synthesis(n):
@@ -164,10 +164,19 @@
     return parts
 
 
+def farthest_first(side):
+    offsets = [
+        (y, x, z, core)
+        for y in range(side) for x in range(side) for z in range(side) for core in range(2)
+    ]
+    hops = lambda offset: sum(min(k, side - k) for k in offset[:3])
+    return sorted(offsets[1:], key=hops, reverse=True)
+
+
 def step_kernel(
     q_hbm, base_hbm, mask_hbm, decay_hbm, to_hbm, from_hbm,
     fwd_hbm, bwd_hbm, sz_hbm, az_hbm, bx_hbm, bz_hbm,
-    stepped_hbm, inverse_ref, growth_ref,
+    stepped_hbm, gram_ref,
     q_v, send, recv, mid, speed, land,
     base_v, base_send, base_recv, mask_v, mask_w, decay_v, to_v, from_v, to_s, from_s,
     fwd_v, bwd_v, sz_v, az_v, bx_v, bz_v,
@@ -213,18 +222,15 @@
 
     barrier = pltpu.get_barrier_semaphore()
 
-    def greet(k, carry):
-        r2, c2 = partner(k)
-        pl.semaphore_signal(barrier, inc=1, device_id=(r2, c2), device_id_type=MESH)
-        return carry
-
-    lax.fori_loop(1, ND, greet, 0)
-
-    def clear(k, carry):
-        recv[pl.ds(PITCH * k + PIECE, PITCH - PIECE), :] = jnp.zeros((PITCH - PIECE, LANES), F32)
-        return carry
-
-    lax.fori_loop(0, HALVES * ND, clear, 0)
+    side = 4
+    ys = [lax.rem(r // side + k, side) * side for k in range(side)]
+    xs = [lax.rem(lax.rem(r, side) + k, side) for k in range(side)]
+    zs = [lax.rem(c // 2 + k, side) * 2 for k in range(side)]
+    cores = [lax.rem(c, 2), 1 - lax.rem(c, 2)]
+    for y, x, z, core in farthest_first(side):
+        pl.semaphore_signal(
+            barrier, inc=1, device_id=(ys[y] + xs[x], zs[z] + cores[core]), device_id_type=MESH
+        )
 
     small[0].wait()
     gap = jnp.zeros((NV - NL, NY), F32)
@@ -285,6 +291,12 @@
     for copy in loads:
         copy.wait()
     pack(0)
+
+    def clear(k, carry):
+        recv[pl.ds(PITCH * k + PIECE, PITCH - PIECE), :] = jnp.zeros((PITCH - PIECE, LANES), F32)
+        return carry
+
+    lax.fori_loop(0, HALVES * ND, clear, 0, unroll=4)
     pl.semaphore_wait(barrier, ND - 1)
     lax.fori_loop(1, ND, send_base, 0)
     send_forward(0)
@@ -393,7 +405,7 @@
                 recv[pl.ds(pl.multiple_of(to, 8), NX), :] = out[:, tile(k)]
             return carry
 
-        lax.fori_loop(0, HI // QUAD, one, 0, unroll=3)
+        lax.fori_loop(0, HI // QUAD, one, 0, unroll=2)
 
     def x_backward(h):
         def one(i, carry):
@@ -416,7 +428,7 @@
                     )
             return carry
 
-        lax.fori_loop(0, NC // 2, one, 0, unroll=2)
+        lax.fori_loop(0, NC // 2, one, 0)
 
     def send_back(h, first, rows, sem):
         def one(k, carry):
@@ -555,25 +567,7 @@
     for k in range(1, NR):
         total += gram_row[k]
 
-    gram = jnp.concatenate(
-        [total] + [pltpu.roll(total, LANES - NV * k, 1) for k in range(1, NV // 8)], axis=0
-    )
-    gram = gram / float(NX * NY * NZ)
-    row32 = lax.broadcasted_iota(jnp.int32, (NV, LANES), 0)
-    work = jnp.where(lane32 < NV, gram, jnp.where(lane32 == row32 + NV, 1.0, 0.0))
-    for k in range(NV - 1):
-        pivot_row = work[k : k + 1, :]
-        factor = work[:, k : k + 1] / work[k : k + 1, k : k + 1]
-        work = work - jnp.where(row32 > k, factor, 0.0) * pivot_row
-    on_diagonal = jnp.where(lane32 == row32, work, 0.0)
-    scale = 1.0 / jnp.sqrt(jnp.sum(on_diagonal, axis=1, keepdims=True))
-    keep = (lane32 >= NV) & (lane32 < 2 * NV)
-    inverse = pltpu.roll(jnp.where(keep, work, 0.0), LANES - NV, 1) * scale
-    inverse_ref[...] = jnp.concatenate(
-        [inverse] + [pltpu.roll(inverse, NV * k, 1) for k in range(1, BLO)], axis=0
-    )
-    diagonal = jnp.sum(on_diagonal, axis=0, keepdims=True)
-    growth_ref[...] = 0.5 * jnp.log(jnp.where(lane32[:1] < NV, diagonal, 1.0))
+    gram_ref[...] = total
 
     drain(base_send, 0, BASE, bs)
     drain(send, 0, HALVES * PIECE, rs)
@@ -585,7 +579,32 @@
         copy.wait()
 
 
-def turn_kernel(stepped_hbm, inverse_ref, growth_ref, out_hbm, growth_out, x_v, y_v, in_sems, out_sems):
+def eliminate(total):
+    lane = lax.broadcasted_iota(jnp.int32, (NV, LANES), 1)
+    row = lax.broadcasted_iota(jnp.int32, (NV, LANES), 0)
+    gram = jnp.concatenate(
+        [total] + [pltpu.roll(total, LANES - NV * k, 1) for k in range(1, NV // 8)], axis=0
+    )
+    gram = gram / float(NX * NY * NZ)
+    work = jnp.where(lane < NV, gram, jnp.where(lane == row + NV, 1.0, 0.0))
+    for k in range(NV - 1):
+        pivot_row = work[k : k + 1, :]
+        factor = work[:, k : k + 1] / work[k : k + 1, k : k + 1]
+        work = work - jnp.where(row > k, factor, 0.0) * pivot_row
+    on_diagonal = jnp.where(lane == row, work, 0.0)
+    scale = 1.0 / jnp.sqrt(jnp.sum(on_diagonal, axis=1, keepdims=True))
+    keep = (lane >= NV) & (lane < 2 * NV)
+    inverse = pltpu.roll(jnp.where(keep, work, 0.0), LANES - NV, 1) * scale
+    inverse = jnp.concatenate(
+        [inverse] + [pltpu.roll(inverse, NV * k, 1) for k in range(1, BLO)], axis=0
+    )
+    diagonal = jnp.sum(on_diagonal, axis=0, keepdims=True)
+    return inverse, 0.5 * jnp.log(diagonal[:, :NV])
+
+
+def turn_kernel(
+    stepped_hbm, gram_hbm, out_hbm, growth_out, x_v, y_v, gram_v, in_sems, out_sems, gram_sem,
+):
     def load(t):
         at = pl.ds(pl.multiple_of(t * LANES, LANES), LANES)
         return pltpu.make_async_copy(stepped_hbm.at[:, :, at], x_v.at[t], in_sems.at[t])
@@ -595,20 +614,19 @@
         return pltpu.make_async_copy(y_v.at[t], out_hbm.at[:, :, at], out_sems.at[t])
 
     count = x_v.shape[0]
+    gram_copy = pltpu.make_async_copy(gram_hbm, gram_v, gram_sem)
+    gram_copy.start()
     for t in range(count):
         load(t).start()
-    top, rest = split2(inverse_ref[...])
-    right = jnp.concatenate([top, rest], axis=0)
-    right = jnp.concatenate([right, right], axis=1)
-    growth_out[...] = growth_ref[:, :NV]
+    gram_copy.wait()
+    inverse, growth_out[...] = eliminate(gram_v[...])
+    right = jnp.concatenate(split2(inverse.T), axis=1)
+    right = jnp.concatenate([right, right], axis=0)
 
     def one(t, carry):
         load(t).wait()
-        nt = (((1,), (1,)), ((), ()))
         rows = x_v[t].reshape(ML * NY, LANES)
-        both = lax.dot_general(
-            jnp.concatenate(split2(rows), axis=1), right, nt, preferred_element_type=F32
-        )
+        both = mm(jnp.concatenate(split2(rows), axis=1), right)
         y_v[t] = (both[:, :LANES] + both[:, LANES:]).reshape(ML, NY, LANES)
         store(t).start()
         return carry
@@ -628,15 +646,14 @@
     anywhere = pl.BlockSpec(memory_space=pl.ANY)
     dma = pltpu.SemaphoreType.DMA
     field = pltpu.VMEM((HALVES * SPAN, LANES), F32)
-    stepped, inverse, growth = pl.pallas_call(
+    stepped, gram = pl.pallas_call(
         step_kernel,
         out_shape=(
             jax.ShapeDtypeStruct(tangents.shape, F32),
-            jax.ShapeDtypeStruct((LANES, LANES), F32),
-            jax.ShapeDtypeStruct((1, LANES), F32),
+            jax.ShapeDtypeStruct((8, LANES), F32),
         ),
         in_specs=[anywhere] * len(inputs),
-        out_specs=(anywhere, vmem, vmem),
+        out_specs=(anywhere, vmem),
         scratch_shapes=[
             pltpu.VMEM(tangents.shape, F32), field, field,
             pltpu.VMEM((HI * NX, LANES), F32),
@@ -675,16 +692,17 @@
             jax.ShapeDtypeStruct(tangents.shape, F32),
             jax.ShapeDtypeStruct((1, NV), F32),
         ),
-        in_specs=[anywhere, vmem, vmem],
+        in_specs=[pl.BlockSpec(memory_space=pltpu.HBM)] * 2,
         out_specs=(anywhere, vmem),
         scratch_shapes=[
             pltpu.VMEM((tiles, ML, NY, LANES), F32),
             pltpu.VMEM((tiles, ML, NY, LANES), F32),
-            dma((tiles,)), dma((tiles,)),
+            pltpu.VMEM((8, LANES), F32),
+            dma((tiles,)), dma((tiles,)), dma,
         ],
-        compiler_params=pltpu.CompilerParams(vmem_limit_bytes=40 * 2**20),
+        compiler_params=pltpu.CompilerParams(vmem_limit_bytes=60 * 2**20),
         name="turn",
-    )(stepped, inverse, growth)
+    )(stepped, gram)
     return vectors, growth.reshape(NV)
 
 

time: 144 us -> 141 us (0.979)
  local copies, waits for them, and re-layouts: 3.84 us -> 0 us
    pallas_call x1, Pallas kernels: 4.34 us -> 8.53 us  [body(): pl.pallas_call(turn_kernel, out_shape=(jax.ShapeDtypeStruct(tangents.shap...]
    unnamed x6 -> x0, local copies, waits for them, and re-layouts: 3.84 us -> none
    pallas_call x1, Pallas kernels: 135 us -> 131 us  [body(): pl.pallas_call(step_kernel, out_shape=(jax.ShapeDtypeStruct(tangents.shap...]
where the time goes in v5:
time: 141 us
  Pallas kernels  140 us (99%)
    pallas_call x1, Pallas kernels, body(): pl.pallas_call(step_kernel, out_shape=(jax.ShapeDtypeStruct(tangents.shap...  131 us
    pallas_call x1, Pallas kernels, body(): pl.pallas_call(turn_kernel, out_shape=(jax.ShapeDtypeStruct(tangents.shap...  8.53 us

profile of v5, /device:TPU:1, one launch (start us, length us, event | category | flops | bytes accessed | tf_op | source)
XLA Modules:
  0.0 140.6 jit_solution(9664940665300920463)
XLA Ops:
  0.6 131.4 %step.1 = (f32[12,128,768]{2,1,0:T(8,128)}, f32[8,128]{1,0:T(8,128)}) custom-call(f32[12,128,768]{2,1,0:T(8,128)} %q_hbm.1, f32[12,24,128]{2,1,0:T(8,128)} %bitcast.3, s32[12,24]{1,0:T(8,128)} %mask_hbm.1, f32[1,128]{1,0:T(1,128)} %bitcast.4, f32[128,128]{1,0:T(8,128)} %to_hbm.1, f32[128,128]{1,0:T(8,128)} %from_hbm.1, ...), custom_call_target="tpu_custom_call" | custom-call | tf_op jit(solution)/shard_map/step/pallas_call | solution.py:649
  132.1 8.5 %turn.1 = (f32[12,128,768]{2,1,0:T(8,128)}, f32[1,32]{1,0:T(1,128)}) custom-call(f32[12,128,768]{2,1,0:T(8,128)} %get-tuple-element.6.stepped_hbm, f32[8,128]{1,0:T(8,128)} %get-tuple-element.7.gram_hbm), custom_call_target="tpu_custom_call" | custom-call | tf_op jit(solution)/shard_map/turn/pallas_call | solution.py:689

commit v6 on v5

--- a/solution.py
+++ b/solution.py
@@ -232,6 +232,64 @@
             barrier, inc=1, device_id=(ys[y] + xs[x], zs[z] + cores[core]), device_id_type=MESH
         )
 
+    def row_of(j, m):
+        return (m, jnp.where(m < 8, 16 + m, 4 + m), 24 + m)[j]
+
+    def half_of(first, second, lane, h):
+        return pair_up(first, second, lane, VH)[h]
+
+    lane8 = lax.broadcasted_iota(jnp.int32, (8, LANES), 1)
+
+    def pack(h):
+        def one(m, carry):
+            for j in range(TILES):
+                for t in range(NY // 8):
+                    rows = slice(8 * t, 8 * t + 8)
+                    send[pl.ds(h * SPAN + 8 * t * PITCH + row_of(j, m), 8, stride=PITCH), :] = half_of(
+                        q_v[m, rows, tile(2 * j)], q_v[m, rows, tile(2 * j + 1)], lane8, h
+                    )
+            return carry
+
+        lax.fori_loop(0, ML, one, 0)
+
+    def send_forward(h):
+        def one(k, carry):
+            r2, c2 = partner(k)
+            pltpu.make_async_remote_copy(
+                send.at[pl.ds(h * SPAN + (r2 * NC + c2) * PITCH, PIECE)],
+                recv.at[pl.ds(h * SPAN + my_slot * PITCH, PIECE)],
+                fs.at[h], fr.at[h], device_id=(r2, c2), device_id_type=MESH,
+            ).start()
+            return carry
+
+        lax.fori_loop(1, ND, one, 0)
+
+    def send_base(k, carry):
+        r2, c2 = partner(k)
+        pltpu.make_async_remote_copy(
+            base_send.at[pl.ds((r2 * NC + c2) * BASE, BASE)],
+            base_recv.at[pl.ds(my_slot * BASE, BASE)],
+            bs, br, device_id=(r2, c2), device_id_type=MESH,
+        ).start()
+        return carry
+
+    def keep_own(dst, to, h):
+        dst[pl.ds(pl.multiple_of(h * SPAN + to * PITCH, 8), PIECE), :] = send[
+            pl.ds(pl.multiple_of(h * SPAN + me * PITCH, 8), PIECE), :
+        ]
+
+    for copy in loads:
+        copy.wait()
+    pack(0)
+
+    def clear(k, carry):
+        recv[pl.ds(PITCH * k + PIECE, PITCH - PIECE), :] = jnp.zeros((PITCH - PIECE, LANES), F32)
+        return carry
+
+    lax.fori_loop(0, HALVES * ND, clear, 0, unroll=4)
+    pl.semaphore_wait(barrier, ND - 1)
+    send_forward(0)
+
     small[0].wait()
     gap = jnp.zeros((NV - NL, NY), F32)
     for high in range(BASE):
@@ -242,64 +300,7 @@
         for t in range(NY // 8):
             base_send[pl.ds(8 * t * BASE + high, 8, stride=BASE), :] = turned[8 * t : 8 * t + 8]
 
-    def row_of(j, m):
-        return (m, jnp.where(m < 8, 16 + m, 4 + m), 24 + m)[j]
-
-    def half_of(first, second, lane, h):
-        return pair_up(first, second, lane, VH)[h]
-
-    lane8 = lax.broadcasted_iota(jnp.int32, (8, LANES), 1)
-
-    def pack(h):
-        def one(m, carry):
-            for j in range(TILES):
-                for t in range(NY // 8):
-                    rows = slice(8 * t, 8 * t + 8)
-                    send[pl.ds(h * SPAN + 8 * t * PITCH + row_of(j, m), 8, stride=PITCH), :] = half_of(
-                        q_v[m, rows, tile(2 * j)], q_v[m, rows, tile(2 * j + 1)], lane8, h
-                    )
-            return carry
-
-        lax.fori_loop(0, ML, one, 0)
-
-    def send_forward(h):
-        def one(k, carry):
-            r2, c2 = partner(k)
-            pltpu.make_async_remote_copy(
-                send.at[pl.ds(h * SPAN + (r2 * NC + c2) * PITCH, PIECE)],
-                recv.at[pl.ds(h * SPAN + my_slot * PITCH, PIECE)],
-                fs.at[h], fr.at[h], device_id=(r2, c2), device_id_type=MESH,
-            ).start()
-            return carry
-
-        lax.fori_loop(1, ND, one, 0)
-
-    def send_base(k, carry):
-        r2, c2 = partner(k)
-        pltpu.make_async_remote_copy(
-            base_send.at[pl.ds((r2 * NC + c2) * BASE, BASE)],
-            base_recv.at[pl.ds(my_slot * BASE, BASE)],
-            bs, br, device_id=(r2, c2), device_id_type=MESH,
-        ).start()
-        return carry
-
-    def keep_own(dst, to, h):
-        dst[pl.ds(pl.multiple_of(h * SPAN + to * PITCH, 8), PIECE), :] = send[
-            pl.ds(pl.multiple_of(h * SPAN + me * PITCH, 8), PIECE), :
-        ]
-
-    for copy in loads:
-        copy.wait()
-    pack(0)
-
-    def clear(k, carry):
-        recv[pl.ds(PITCH * k + PIECE, PITCH - PIECE), :] = jnp.zeros((PITCH - PIECE, LANES), F32)
-        return carry
-
-    lax.fori_loop(0, HALVES * ND, clear, 0, unroll=4)
-    pl.semaphore_wait(barrier, ND - 1)
     lax.fori_loop(1, ND, send_base, 0)
-    send_forward(0)
     pack(1)
     send_forward(1)
     base_recv[pl.ds(my_slot * BASE, BASE), :] = base_send[pl.ds(me * BASE, BASE), :]

time: 141 us -> 144 us (1.021)
  Pallas kernels: 140 us -> 143 us
    pallas_call x1, Pallas kernels: 131 us -> 135 us  [body(): pl.pallas_call(step_kernel, out_shape=(jax.ShapeDtypeStruct(tangents.shap...]
where the time goes in v6:
time: 144 us
  Pallas kernels  143 us (99%)
    pallas_call x1, Pallas kernels, body(): pl.pallas_call(step_kernel, out_shape=(jax.ShapeDtypeStruct(tangents.shap...  135 us
    pallas_call x1, Pallas kernels, body(): pl.pallas_call(turn_kernel, out_shape=(jax.ShapeDtypeStruct(tangents.shap...  8.53 us

profile of v6, /device:TPU:1, one launch (start us, length us, event | category | flops | bytes accessed | tf_op | source)
XLA Modules:
  0.0 143.8 jit_solution(9983611955256231875)
XLA Ops:
  0.6 134.6 %step.1 = (f32[12,128,768]{2,1,0:T(8,128)}, f32[8,128]{1,0:T(8,128)}) custom-call(f32[12,128,768]{2,1,0:T(8,128)} %q_hbm.1, f32[12,24,128]{2,1,0:T(8,128)} %bitcast.3, s32[12,24]{1,0:T(8,128)} %mask_hbm.1, f32[1,128]{1,0:T(1,128)} %bitcast.4, f32[128,128]{1,0:T(8,128)} %to_hbm.1, f32[128,128]{1,0:T(8,128)} %from_hbm.1, ...), custom_call_target="tpu_custom_call" | custom-call | tf_op jit(solution)/shard_map/step/pallas_call | solution.py:650
  135.3 8.5 %turn.1 = (f32[12,128,768]{2,1,0:T(8,128)}, f32[1,32]{1,0:T(1,128)}) custom-call(f32[12,128,768]{2,1,0:T(8,128)} %get-tuple-element.6.stepped_hbm, f32[8,128]{1,0:T(8,128)} %get-tuple-element.7.gram_hbm), custom_call_target="tpu_custom_call" | custom-call | tf_op jit(solution)/shard_map/turn/pallas_call | solution.py:690
